TPU v7x, 32 devices: a whole 2x2x4 slice. The times are simulated.
32 devices in a mesh: tm: 4 (over y, x), space: 8 (over z, core).
Axes of the slice: x: 2, y: 2, z: 4, core: 2. Of those that a mesh axis runs over, the one named last changes fastest.
Arguments:
- residual: float32 [64, 64, 8, 128], P('tm', 'space'), may hold values from -24 to 24
- capacity: float32 [64, 8, 128], P('space'), may hold values from 0.25 to 4
Outputs:
- preconditioned: float32 [64, 64, 8, 128], P('tm', 'space')
All inputs are finite; a program needn't handle non-finite values.
Results may differ from a plain program's by a relative error of at most 0.0003.
Values sent between devices are 32-bit elements; how exact they have to be, the bound alone decides.
A program may use at most 64 MiB of HBM per device.

v0:
```python
import functools
import math

import jax
import jax.numpy as jnp
import numpy as np
from jax import lax
from jax.experimental import pallas as pl
from jax.experimental.pallas import tpu as pltpu
from jax.sharding import PartitionSpec as P

GRID_DEPTH = 4
SMOOTH = 2
COARSE_SWEEPS = 6


ALPHA_CORNER = 0.01
STEP_SIZE = 0.5
DIFFUSE = 2.0
ADVECT = (0.2, -0.15, 0.1)
OMEGA = 0.7
HIGHEST = lax.Precision.HIGHEST


def extended(array, sides, width):
    for axis, dim in sides:
        peers, length = (lax.axis_size(axis), array.shape[dim])
        up = [(i, (i + 1) % peers) for i in range(peers - 1)]
        down = [(j, i) for i, j in up]
        last = lax.slice_in_dim(array, length - width, length, axis=dim)
        initial = lax.slice_in_dim(array, 0, width, axis=dim)
        before = lax.ppermute(last, axis, up)
        after = lax.ppermute(initial, axis, down)
        array = jnp.concatenate([before, array, after], axis=dim)
    return array


def level_coefficients(per_level_values):
    spread = DIFFUSE / 4.0**per_level_values
    drifts = tuple((component / 2.0**per_level_values for component in ADVECT))
    return (spread, drifts)


def pad_second(volume, position):
    widths = [(0, 0)] * volume.ndim
    widths[position] = (1, 1)
    return jnp.pad(volume, widths)


def apply_operator(padded, current_capacity, spectral_shifts, per_level_values):
    spread, drifts = level_coefficients(per_level_values)
    centre = padded[:, :, 1:-1]
    upper_first = padded[:, :, 2:]
    lower_first = padded[:, :, :-2]
    wide_second = pad_second(centre, 3)
    upper_second = wide_second[:, :, :, 2:]
    lower_second = wide_second[:, :, :, :-2]
    wide_third = pad_second(centre, 4)
    upper_third = wide_third[:, :, :, :, 2:]
    lower_third = wide_third[:, :, :, :, :-2]
    stencil = spread * (
        6.0 * centre
        - upper_first
        - lower_first
        - upper_second
        - lower_second
        - upper_third
        - lower_third
    )
    stencil = (
        stencil
        + drifts[0] * (upper_first - lower_first)
        + drifts[1] * (upper_second - lower_second)
        + drifts[2] * (upper_third - lower_third)
    )
    first_shift, second_shift, third_shift = spectral_shifts
    real_part = centre[0]
    imag_part = centre[1]
    shifted = jnp.stack(
        [
            current_capacity * (first_shift * real_part - second_shift * imag_part),
            current_capacity * (second_shift * real_part + third_shift * imag_part),
        ]
    )
    return stencil + shifted


def inverse_diagonal(current_capacity, spectral_shifts, per_level_values):
    spread, drifts = level_coefficients(per_level_values)
    first_shift, second_shift, third_shift = spectral_shifts
    top_left = current_capacity * first_shift + 6.0 * spread
    coupling = current_capacity * second_shift
    bottom_right = current_capacity * third_shift + 6.0 * spread
    determinant = top_left * bottom_right + coupling * coupling
    return (bottom_right / determinant, coupling / determinant, top_left / determinant)


def damped_update(residual_now, inverse):
    diagonal_a, diagonal_b, diagonal_c = inverse
    return OMEGA * jnp.stack(
        [
            diagonal_a * residual_now[0] + diagonal_b * residual_now[1],
            diagonal_c * residual_now[1] - diagonal_b * residual_now[0],
        ]
    )


def restrict_to_coarse(volume):
    leading = volume.shape[:-3]
    first_extent, second_extent, third_extent = volume.shape[-3:]
    blocks = volume.reshape(
        leading + (first_extent // 2, 2, second_extent // 2, 2, third_extent // 2, 2)
    )
    lead_count = len(leading)
    return jnp.mean(blocks, axis=(lead_count + 1, lead_count + 3, lead_count + 5))


def prolong_cells(volume):
    leading = volume.shape[:-3]
    first_extent, second_extent, third_extent = volume.shape[-3:]
    expanded = jnp.broadcast_to(
        volume[..., :, None, :, None, :, None],
        leading + (first_extent, 2, second_extent, 2, third_extent, 2),
    )
    return expanded.reshape(leading + (2 * first_extent, 2 * second_extent, 2 * third_extent))


def shift_values(frequency, length):
    ratio_step = ALPHA_CORNER ** (1.0 / length)
    phases = 2.0 * math.pi / length * frequency.astype(jnp.float32)
    first_shift = (1.0 - ratio_step * jnp.cos(phases)) / STEP_SIZE
    second_shift = ratio_step * jnp.sin(phases) / STEP_SIZE
    leading = frequency == 0
    second_shift = jnp.where(leading, 0.0, second_shift)
    third_shift = jnp.where(leading, (1.0 + ratio_step) / STEP_SIZE, first_shift)
    return tuple(
        (column.reshape(-1, 1, 1, 1) for column in (first_shift, second_shift, third_shift))
    )


def phase_grid(row_count, length):
    integers = (
        jnp.arange(row_count, dtype=jnp.int32)[:, None]
        * jnp.arange(length, dtype=jnp.int32)[None, :]
        % length
    )
    return 2.0 * math.pi / length * integers.astype(jnp.float32)


def pad_faces(volume):
    return extended(volume, (("space", 2),), 1)


def multigrid_cycle(
    per_level_values,
    forcing_term,
    capacity_fields,
    spectral_shifts,
    shared_values,
    assemble_level,
    assemble_parts,
):
    current_capacity = capacity_fields[per_level_values]
    inverse = inverse_diagonal(current_capacity, spectral_shifts, per_level_values)
    coarsest = per_level_values == GRID_DEPTH - 1
    current = damped_update(forcing_term, inverse)
    for repeat in range((COARSE_SWEEPS if coarsest else SMOOTH) - 1):
        current = current + damped_update(
            forcing_term
            - apply_operator(
                pad_faces(current), current_capacity, spectral_shifts, per_level_values
            ),
            inverse,
        )
    if coarsest:
        return current
    coarse_right_hand = restrict_to_coarse(
        forcing_term
        - apply_operator(pad_faces(current), current_capacity, spectral_shifts, per_level_values)
    )
    coarse_solution = multigrid_cycle(
        per_level_values + 1,
        coarse_right_hand,
        capacity_fields,
        spectral_shifts,
        shared_values,
        assemble_level,
        assemble_parts,
    )
    current = current + prolong_cells(coarse_solution)
    for repeat in range(SMOOTH):
        current = current + damped_update(
            forcing_term
            - apply_operator(
                pad_faces(current), current_capacity, spectral_shifts, per_level_values
            ),
            inverse,
        )
    return current


def on_device(residual, capacity):
    steps_here, thickness, extent_second, extent_third = residual.shape
    length = lax.axis_size("tm") * steps_here
    ratio_step = ALPHA_CORNER ** (1.0 / length)
    moments = (lax.axis_index("tm") * steps_here + jnp.arange(steps_here, dtype=jnp.int32)).astype(
        jnp.float32
    )
    scaled = (residual * jnp.power(ratio_step, moments)[:, None, None, None]).reshape(
        steps_here, -1
    )
    series = lax.all_to_all(scaled, "tm", split_axis=1, concat_axis=0, tiled=True)
    all_weights = jnp.power(ratio_step, jnp.arange(length, dtype=jnp.float32))
    alternate = 1.0 - 2.0 * (jnp.arange(length, dtype=jnp.int32) % 2).astype(jnp.float32)
    capacity_fields = [capacity]
    for per_level_values in range(1, GRID_DEPTH):
        capacity_fields.append(restrict_to_coarse(capacity_fields[-1]))
    halves = length // 2
    phases = phase_grid(halves, length)
    first_row = jnp.arange(halves, dtype=jnp.int32)[:, None] == 0
    forward = jnp.concatenate(
        [jnp.cos(phases), jnp.where(first_row, alternate[None, :], -jnp.sin(phases))], axis=0
    )
    spectrum = jnp.dot(forward, series, precision=HIGHEST).reshape(2, halves, -1)
    received = lax.all_to_all(spectrum, "tm", split_axis=1, concat_axis=2, tiled=True)
    slot_count = steps_here // 2
    frequency = lax.axis_index("tm") * slot_count + jnp.arange(slot_count, dtype=jnp.int32)
    spectral_shifts = shift_values(frequency, length)
    field_list = received.reshape(2, slot_count, thickness, extent_second, extent_third)
    solved_fields = multigrid_cycle(
        0, field_list, capacity_fields, spectral_shifts, False, GRID_DEPTH, None
    )
    flattened = solved_fields.reshape(2, slot_count, -1)
    returned = lax.all_to_all(flattened, "tm", split_axis=2, concat_axis=1, tiled=True)
    halves = length // 2
    phases = jnp.transpose(phase_grid(halves, length))
    first_column = jnp.arange(halves, dtype=jnp.int32)[None, :] == 0
    real_columns = jnp.where(first_column, 1.0, 2.0 * jnp.cos(phases)) / length
    imag_columns = jnp.where(first_column, alternate[:, None], -2.0 * jnp.sin(phases)) / length
    inverse_table = jnp.concatenate([real_columns, imag_columns], axis=1)
    values = jnp.dot(
        inverse_table,
        returned.reshape(returned.shape[0] * returned.shape[1], -1),
        precision=HIGHEST,
    )
    values = values / all_weights[:, None]
    result = lax.all_to_all(values, "tm", split_axis=0, concat_axis=1, tiled=True)
    return result.reshape(residual.shape)


MESH = pl.DeviceIdType.MESH


def real_transform(values):
    count = len(values)
    if count == 1:
        return [(values[0], None)]
    evens, odds = real_transform(values[0::2]), real_transform(values[1::2])
    half = count // 2
    if count == 2:
        return [(evens[0][0] + odds[0][0], None), (evens[0][0] - odds[0][0], None)]
    found = [None] * (half + 1)
    found[0] = (evens[0][0] + odds[0][0], None)
    found[half] = (evens[0][0] - odds[0][0], None)
    found[half // 2] = (evens[half // 2][0], -odds[half // 2][0])
    for k in range(1, half // 2):
        cosine, sine = math.cos(2 * math.pi * k / count), -math.sin(2 * math.pi * k / count)
        (er, ei), (or_, oi) = evens[k], odds[k]
        tr, ti = cosine * or_ - sine * oi, cosine * oi + sine * or_
        found[k] = (er + tr, ei + ti)
        found[half - k] = (er - tr, ti - ei)
    return found


def real_inverse(modes):
    half = len(modes) - 1
    if half == 0:
        return [modes[0][0]]
    count = 2 * half
    if half == 1:
        return [modes[0][0] + modes[1][0], modes[0][0] - modes[1][0]]
    evens, odds = [None] * (half // 2 + 1), [None] * (half // 2 + 1)
    evens[0] = (modes[0][0] + modes[half][0], None)
    odds[0] = (modes[0][0] - modes[half][0], None)
    middle = modes[half // 2]
    evens[half // 2] = (2.0 * middle[0], None)
    odds[half // 2] = (-2.0 * middle[1], None)
    for k in range(1, half // 2):
        cosine, sine = math.cos(2 * math.pi * k / count), math.sin(2 * math.pi * k / count)
        (ar, ai), (br, bi) = modes[k], modes[half - k]
        dr, di = ar - br, ai + bi
        evens[k] = (ar + br, ai - bi)
        odds[k] = (cosine * dr - sine * di, cosine * di + sine * dr)
    first, second = real_inverse(evens), real_inverse(odds)
    return [part for pair in zip(first, second) for part in pair]


def pair_sum(value, distance):
    for axis in (-2, -1):
        dim = value.ndim + axis
        extent = value.shape[dim]
        upper = pltpu.roll(value, extent - distance, dim)
        lower = pltpu.roll(value, distance, dim)
        place = lax.broadcasted_iota(jnp.int32, value.shape, dim)
        value = value + jnp.where((place // distance) % 2 == 0, upper, lower)
    return value


def block_mean(value, distance):
    shape = (value.shape[0] // 2, 2) + value.shape[1:]
    paired = value.reshape(shape)
    return 0.125 * pair_sum(paired[:, 0] + paired[:, 1], distance)


def neighbour_weights(level, shape):
    spread, drifts = level_coefficients(level)
    distance = 2**level
    along_first = (drifts[0] - spread, -drifts[0] - spread)
    masked = []
    for dim in (0, 1):
        place = lax.broadcasted_iota(jnp.int32, shape, dim)
        upper = jnp.where(place < shape[dim] - distance, drifts[dim + 1] - spread, 0.0)
        lower = jnp.where(place >= distance, -drifts[dim + 1] - spread, 0.0)
        masked.append((upper, lower))
    return along_first, masked, distance


def neighbours(wide, weights):
    along_first, masked, distance = weights
    centre = wide[1:-1]
    total = along_first[0] * wide[2:] + along_first[1] * wide[:-2]
    for dim in (0, 1):
        extent = centre.shape[dim + 1]
        if distance >= extent:
            continue
        upper, lower = masked[dim]
        total = total + upper[None] * pltpu.roll(centre, extent - distance, dim + 1)
        total = total + lower[None] * pltpu.roll(centre, distance, dim + 1)
    return total


def blocks_of(extent, largest, body):
    block = min(extent, largest)

    def step(i, carry):
        body(pl.multiple_of(i * block, block), block)
        return carry

    if extent == block:
        body(0, block)
    else:
        lax.fori_loop(0, extent // block, step, 0)


BLOCK = 64


def prepare_level(level, caps, inverses, shifts):
    spread, unused = level_coefficients(level)
    s1, s2, s3 = shifts

    def body(start, block):
        cap = caps[level][pl.ds(start, block)]
        top, coupling, bottom = cap * s1 + 6.0 * spread, cap * s2, cap * s3 + 6.0 * spread
        scale = OMEGA / (top * bottom + coupling * coupling)
        inverses[level][pl.ds(start, block), 0] = bottom * scale
        inverses[level][pl.ds(start, block), 1] = coupling * scale
        inverses[level][pl.ds(start, block), 2] = top * scale
        if level + 1 < GRID_DEPTH:
            half = block // 2
            caps[level + 1][pl.ds(start // 2, half)] = block_mean(cap, 2**level)

    blocks_of(caps[level].shape[0], BLOCK, body)


def smooth_first(forcing, target, inverse):
    def body(start, block):
        here = pl.ds(start, block)
        a, b, c = inverse[here, 0], inverse[here, 1], inverse[here, 2]
        re, im = forcing[here, 0], forcing[here, 1]
        there = pl.ds(start + 1, block)
        target[there, 0] = a * re + b * im
        target[there, 1] = c * im - b * re

    blocks_of(forcing.shape[0], BLOCK, body)


def smooth(forcing, source, target, inverse, weights, offset=1, coarse=None):
    def body(start, block):
        here = pl.ds(start, block)
        wide_re = source[pl.ds(start, block + 2), 0]
        wide_im = source[pl.ds(start, block + 2), 1]
        r0 = forcing[here, 0] - neighbours(wide_re, weights)
        r1 = forcing[here, 1] - neighbours(wide_im, weights)
        a, b, c = inverse[here, 0], inverse[here, 1], inverse[here, 2]
        there = pl.ds(start + offset, block)
        target[there, 0] = (1.0 - OMEGA) * wide_re[1:-1] + (a * r0 + b * r1)
        target[there, 1] = (1.0 - OMEGA) * wide_im[1:-1] + (c * r1 - b * r0)

    blocks_of(forcing.shape[0], BLOCK, body)


def restrict_residual(level, forcing, source, cap, shifts, weights, target):
    spread, unused = level_coefficients(level)
    s1, s2, s3 = shifts

    def body(start, block):
        here = pl.ds(start, block)
        wide_re = source[pl.ds(start, block + 2), 0]
        wide_im = source[pl.ds(start, block + 2), 1]
        re, im = wide_re[1:-1], wide_im[1:-1]
        field = cap[here]
        r0 = forcing[here, 0] - neighbours(wide_re, weights)
        r1 = forcing[here, 1] - neighbours(wide_im, weights)
        r0 = r0 - (6.0 * spread * re + field * (s1 * re - s2 * im))
        r1 = r1 - (6.0 * spread * im + field * (s2 * re + s3 * im))
        half = pl.ds(start // 2, block // 2)
        target[half, 0] = block_mean(r0, 2**level)
        target[half, 1] = block_mean(r1, 2**level)

    blocks_of(forcing.shape[0], BLOCK, body)


def add_coarse(target, coarse):
    def body(start, block):
        half = block // 2
        for part in (0, 1):
            extra = coarse[pl.ds(start // 2 + 1, half), part]
            spread = jnp.broadcast_to(extra[:, None], (half, 2) + extra.shape[1:])
            there = pl.ds(start + 1, block)
            target[there, part] = target[there, part] + spread.reshape((block,) + extra.shape[1:])

    blocks_of(target.shape[0] - 2, BLOCK, body)


def cycle(level, forcings, caps, inverses, firsts, seconds, shifts, result):
    forcing, inverse = forcings[level], inverses[level]
    here, other = firsts[level], seconds[level]
    weights = neighbour_weights(level, forcing.shape[-2:])
    coarsest = level == GRID_DEPTH - 1
    smooth_first(forcing, here, inverse)
    for repeat in range((COARSE_SWEEPS if coarsest else SMOOTH) - 1):
        smooth(forcing, here, other, inverse, weights)
        here, other = other, here
    if coarsest:
        return here
    restrict_residual(level, forcing, here, caps[level], shifts, weights, forcings[level + 1])
    coarse = cycle(level + 1, forcings, caps, inverses, firsts, seconds, shifts, None)
    add_coarse(here, coarse)
    for repeat in range(SMOOTH):
        last = repeat == SMOOTH - 1 and result is not None
        target = result if last else other
        smooth(forcing, here, target, inverse, weights, offset=0 if last else 1)
        here, other = target, here
    return here


def whole_kernel(groups, slabs, shift_table, residual_hbm, capacity_hbm, out_ref, *scratch):
    (series, spectrum, returned, values, result) = scratch[:5]
    residual_ref = scratch[-1]
    scratch = scratch[:-1]
    depth = GRID_DEPTH
    forcings = scratch[5 : 5 + depth]
    caps = scratch[5 + depth : 5 + 2 * depth]
    inverses = scratch[5 + 2 * depth : 5 + 3 * depth]
    firsts = scratch[5 + 3 * depth : 5 + 4 * depth]
    seconds = scratch[5 + 4 * depth : 5 + 5 * depth]
    send1, recv1, send2, recv2, send3, recv3, send4, recv4, own, sendc, recvc, ready = scratch[
        5 + 5 * depth :
    ]
    steps, thick = residual_ref.shape[:2]
    planes = thick // groups
    length = groups * steps
    devices = groups * slabs
    ratio_step = ALPHA_CORNER ** (1.0 / length)
    mine, slab = lax.axis_index("tm"), lax.axis_index("space")
    me = mine * slabs + slab
    base = slab * thick + mine * planes

    def peer_of(k):
        to_tm = lax.rem(mine + k, groups)
        to_space = lax.rem(slab + k // groups, slabs)
        return to_tm * slabs + to_space, to_tm, to_space

    own_slab = pl.ds(slab * thick, thick)
    take_residual = pltpu.make_async_copy(residual_hbm, residual_ref, own.at[3 * planes])
    take_capacity = pltpu.make_async_copy(
        capacity_hbm, caps[0].at[own_slab], own.at[3 * planes + 1]
    )
    take_residual.start()
    take_capacity.start()
    barrier = pltpu.get_barrier_semaphore()

    partner = slab + 1 - 2 * lax.rem(slab, 2)
    below, above = slab >= 2, slab < slabs - 2
    sides = jnp.where(below, 1, 0) + jnp.where(above, 1, 0)

    def tell_sides(semaphore):
        for there, step in ((below, -2), (above, 2)):

            @pl.when(there)
            def _():
                pl.semaphore_signal(
                    semaphore, inc=1, device_id=(mine, slab + step), device_id_type=MESH
                )

    for d in range(1, groups):
        pl.semaphore_signal(
            barrier, inc=1, device_id=(lax.rem(mine + d, groups), slab), device_id_type=MESH
        )
    tell_sides(barrier)
    pl.semaphore_signal(barrier, inc=1, device_id=(mine, partner), device_id_type=MESH)
    for level in range(depth):
        for buffer in (firsts[level], seconds[level]):
            empty = jnp.zeros(buffer.shape[1:], jnp.float32)
            buffer[0] = empty
            buffer[buffer.shape[0] - 1] = empty
    take_residual.wait()
    pl.semaphore_wait(barrier, groups + sides)

    first_sends = []
    for p in range(planes):
        for d in range(1, groups):
            to_tm = lax.rem(mine + d, groups)
            copy = pltpu.make_async_remote_copy(
                src_ref=residual_ref.at[:, to_tm * planes + p],
                dst_ref=series.at[p, pl.ds(mine * steps, steps)],
                send_sem=send1.at[p, d],
                recv_sem=recv1.at[p, d],
                device_id=(to_tm, slab),
                device_id_type=MESH,
            )
            copy.start()
            first_sends.append(copy)
    own_steps = []
    for p in range(planes):
        copy = pltpu.make_async_copy(
            residual_ref.at[:, mine * planes + p],
            series.at[p, pl.ds(mine * steps, steps)],
            own.at[p],
        )
        copy.start()
        own_steps.append(copy)

    for turn in range(slabs // 2 - 1):
        tell_sides(ready.at[turn])
        pl.semaphore_wait(ready.at[turn], sides)
    last = slabs // 2 - 1
    pl.semaphore_signal(ready.at[last], inc=1, device_id=(mine, partner), device_id_type=MESH)
    pl.semaphore_wait(ready.at[last], 1)

    take_capacity.wait()
    cap_sends = []
    for d in range(1, slabs // 2):
        copy = pltpu.make_async_remote_copy(
            src_ref=caps[0].at[own_slab],
            dst_ref=caps[0].at[own_slab],
            send_sem=sendc.at[d],
            recv_sem=recvc.at[d],
            device_id=(mine, lax.rem(slab + 2 * d, slabs)),
            device_id_type=MESH,
        )
        copy.start()
        cap_sends.append(copy)

    def forward_cap(d):
        index = lax.rem(slab + slabs - 2 * d, slabs)
        rows = pl.ds(index * thick, thick)
        copy = pltpu.make_async_remote_copy(
            src_ref=caps[0].at[rows],
            dst_ref=caps[0].at[rows],
            send_sem=sendc.at[slabs // 2 + d],
            recv_sem=recvc.at[slabs // 2 + d],
            device_id=(mine, partner),
            device_id_type=MESH,
        )
        copy.start()
        return copy

    cap_forwards = [forward_cap(0)]

    def spread_mode(k, p):
        peer, to_tm, to_space = peer_of(k)
        return pltpu.make_async_remote_copy(
            src_ref=spectrum.at[p, peer],
            dst_ref=forcings[0].at[base + p],
            send_sem=send2.at[p],
            recv_sem=recv2.at[p],
            device_id=(to_tm, to_space),
            device_id_type=MESH,
        )

    own_modes = []
    for p in range(planes):
        own_steps[p].wait()
        for d in range(1, groups):
            first_sends[p * (groups - 1) + d - 1].wait_recv()
        modes = real_transform([ratio_step**t * series[p, t] for t in range(length)])
        spectrum[p, 0, 0] = modes[0][0]
        spectrum[p, 0, 1] = modes[length // 2][0]
        for k in range(1, length // 2):
            spectrum[p, k, 0] = modes[k][0]
            spectrum[p, k, 1] = modes[k][1]

        def start_mode(k, carry):
            spread_mode(k, p).start()
            return carry

        lax.fori_loop(1, devices, start_mode, 0)
        copy = pltpu.make_async_copy(
            spectrum.at[p, me], forcings[0].at[base + p], own.at[planes + p]
        )
        copy.start()
        own_modes.append(copy)

    for d in range(1, slabs // 2):
        cap_sends[d - 1].wait_recv()
        cap_forwards.append(forward_cap(d))
    for copy in cap_forwards:
        copy.wait_recv()
    shifts = []
    for column in range(3):
        value = jnp.float32(shift_table[0, column])
        for k in range(1, devices):
            value = jnp.where(me == k, jnp.float32(shift_table[k, column]), value)
        shifts.append(value)
    for level in range(depth):
        prepare_level(level, caps, inverses, shifts)

    def all_but_one(array, semaphore):
        part = array.at[pl.ds(0, devices - 1)]
        return pltpu.make_async_copy(part, part, semaphore)

    for p in range(planes):
        own_modes[p].wait()
        all_but_one(forcings[0], recv2.at[p]).wait()

    cycle(0, forcings, caps, inverses, firsts, seconds, shifts, result)

    def send_back(k, p):
        peer, to_tm, to_space = peer_of(k)
        return pltpu.make_async_remote_copy(
            src_ref=result.at[to_space * thick + to_tm * planes + p],
            dst_ref=returned.at[p, me],
            send_sem=send3.at[p],
            recv_sem=recv3.at[p],
            device_id=(to_tm, to_space),
            device_id_type=MESH,
        )

    own_back = []
    for p in range(planes):

        def start_back(k, carry):
            send_back(k, p).start()
            return carry

        lax.fori_loop(1, devices, start_back, 0)
        copy = pltpu.make_async_copy(
            result.at[base + p], returned.at[p, me], own.at[2 * planes + p]
        )
        copy.start()
        own_back.append(copy)

    last_copies = []
    for p in range(planes):
        own_back[p].wait()
        all_but_one(returned.at[p], recv3.at[p]).wait()
        modes = [(returned[p, 0, 0], None)]
        modes += [(returned[p, k, 0], returned[p, k, 1]) for k in range(1, length // 2)]
        modes += [(returned[p, 0, 1], None)]
        for t, value in enumerate(real_inverse(modes)):
            values[p, t] = value * (ratio_step**-t / length)
        for d in range(1, groups):
            to_tm = lax.rem(mine + d, groups)
            copy = pltpu.make_async_remote_copy(
                src_ref=values.at[p, pl.ds(to_tm * steps, steps)],
                dst_ref=out_ref.at[:, mine * planes + p],
                send_sem=send4.at[p, d],
                recv_sem=recv4.at[p, d],
                device_id=(to_tm, slab),
                device_id_type=MESH,
            )
            copy.start()
            last_copies.append(copy)
        out_ref[:, mine * planes + p] = values[p, pl.ds(mine * steps, steps)]

    for copy in last_copies:
        copy.wait()
    for copy in first_sends + cap_sends + cap_forwards:
        copy.wait_send()
    for p in range(planes):
        all_but_one(spectrum.at[p], send2.at[p]).wait()
        all_but_one(result, send3.at[p]).wait()


def level_extents(extent):
    return [extent // 2**level for level in range(GRID_DEPTH)]


def fused(groups, slabs, residual, capacity):
    steps, thick, second, third = residual.shape
    length, devices = groups * steps, groups * slabs
    planes, extent = thick // groups, slabs * thick
    tile = (second, third)
    ratio_step = ALPHA_CORNER ** (1.0 / length)
    angle = 2.0 * np.pi / length * np.arange(devices)
    table = np.stack(
        [
            (1.0 - ratio_step * np.cos(angle)) / STEP_SIZE,
            ratio_step * np.sin(angle) / STEP_SIZE,
            (1.0 - ratio_step * np.cos(angle)) / STEP_SIZE,
        ],
        axis=1,
    )
    table[0, 1], table[0, 2] = 0.0, (1.0 + ratio_step) / STEP_SIZE
    extents = level_extents(extent)
    vmem = lambda *shape: pltpu.VMEM(shape + tile, jnp.float32)
    sems = lambda *shape: pltpu.SemaphoreType.DMA(shape)
    scratch = [
        vmem(planes, length),
        vmem(planes, devices, 2),
        vmem(planes, devices, 2),
        vmem(planes, length),
        vmem(extent, 2),
        *[vmem(n, 2) for n in extents],
        *[vmem(n) for n in extents],
        *[vmem(n, 3) for n in extents],
        *[vmem(n + 2, 2) for n in extents],
        *[vmem(n + 2, 2) for n in extents],
        sems(planes, groups),
        sems(planes, groups),
        sems(planes),
        sems(planes),
        sems(planes),
        sems(planes),
        sems(planes, groups),
        sems(planes, groups),
        sems(3 * planes + 2),
        sems(slabs),
        sems(slabs),
        pltpu.SemaphoreType.REGULAR((slabs // 2,)),
        pltpu.VMEM(residual.shape, jnp.float32),
    ]
    return pl.pallas_call(
        functools.partial(whole_kernel, groups, slabs, table),
        out_shape=jax.ShapeDtypeStruct(residual.shape, jnp.float32),
        in_specs=[
            pl.BlockSpec(memory_space=pltpu.HBM),
            pl.BlockSpec(memory_space=pltpu.HBM),
        ],
        out_specs=pl.BlockSpec(memory_space=pltpu.VMEM),
        scratch_shapes=scratch,
        compiler_params=pltpu.CompilerParams(
            collective_id=0, has_side_effects=True, vmem_limit_bytes=32 * 2**20
        ),
    )(residual, capacity)


def fits_fused(groups, slabs, residual):
    steps, thick, second, third = residual.shape
    length = groups * steps
    power = length & (length - 1) == 0
    return (
        power
        and groups * slabs == length // 2
        and slabs % 2 == 0
        and thick % groups == 0
        and all(n % 2 == 0 and n % min(n, BLOCK) == 0 for n in level_extents(slabs * thick))
        and (second, third) == (8, 128)
    )


def either(residual, capacity):
    groups, slabs = lax.axis_size("tm"), lax.axis_size("space")
    if fits_fused(groups, slabs, residual):
        return fused(groups, slabs, residual, capacity)
    return on_device(residual, capacity)


def solution(mesh):
    return jax.shard_map(
        either,
        mesh=mesh,
        in_specs=(P("tm", "space", None, None), P("space", None, None)),
        out_specs=P("tm", "space", None, None),
        check_vma=False,
    )
```

profile of v0, /device:TPU:1, one launch (start us, length us, event | category | flops | bytes accessed | tf_op | source)
XLA Modules:
  0.0 48.7 jit_solution(4270941216031411824)
XLA Ops:
  0.0 0.0 copy-start
  0.0 1.0 %copy-done = f32[16,8,8,128]{3,2,1,0:T(8,128)S(1)} copy-done((f32[16,8,8,128]{3,2,1,0:T(8,128)S(1)}, f32[16,8,8,128]{3,2,1,0:T(8,128)}, u32[]{:S(2)}) %copy-start) | copy-done | bytes 524312
  1.0 0.0 copy-start.1
  1.0 0.8 %copy-done.1 = f32[8,8,128]{2,1,0:T(8,128)S(1)} copy-done((f32[8,8,128]{2,1,0:T(8,128)S(1)}, f32[8,8,128]{2,1,0:T(8,128)}, u32[]{:S(2)}) %copy-start.1) | copy-done | bytes 32792
  1.8 46.0 %shard_map.28 = f32[16,8,8,128]{3,2,1,0:T(8,128)S(1)} custom-call(f32[16,8,8,128]{3,2,1,0:T(8,128)S(1)} %copy-done, f32[8,8,128]{2,1,0:T(8,128)S(1)} %copy-done.1), custom_call_target="tpu_custom_call" | custom-call | tf_op jit(solution)/shard_map/pallas_call | solution.py:745
  47.9 0.8 %copy.4 = f32[16,8,8,128]{3,2,1,0:T(8,128)} copy(f32[16,8,8,128]{3,2,1,0:T(8,128)S(1)} %shard_map.28) | data formatting | bytes 1048576
Async XLA Ops:
  0.0 1.0 %copy-start = (f32[16,8,8,128]{3,2,1,0:T(8,128)S(1)}, f32[16,8,8,128]{3,2,1,0:T(8,128)}, u32[]{:S(2)}) copy-start(f32[16,8,8,128]{3,2,1,0:T(8,128)} %residual_hbm.1) | copy-start | bytes 1572868
  1.0 0.8 %copy-start.1 = (f32[8,8,128]{2,1,0:T(8,128)S(1)}, f32[8,8,128]{2,1,0:T(8,128)}, u32[]{:S(2)}) copy-start(f32[8,8,128]{2,1,0:T(8,128)} %capacity_hbm.1) | copy-start | bytes 98308
where the time goes:
time: 49.3 us; the launch traced here: 48.7 us
  Pallas kernels  46 us (93%)
  local copies, waits for them, and re-layouts  2.59 us (5%)
    pallas_call x1, Pallas kernels, fused(): pl.pallas_call(functools.partial(whole_kernel, groups, slabs, table), out...  46 us
    unnamed x5, local copies, waits for them, and re-layouts  2.59 us

commit v1 on v0

--- a/solution.py
+++ b/solution.py
@@ -455,243 +455,674 @@
     return here
 
 
+def complex_transform(values, sign):
+    count = len(values)
+    if count == 1:
+        return values
+    evens, odds = complex_transform(values[0::2], sign), complex_transform(values[1::2], sign)
+    first, second = [], []
+    for k in range(count // 2):
+        (er, ei), (or_, oi) = evens[k], odds[k]
+        tr, ti = turned(or_, oi, k, count, sign)
+        first.append((er + tr, ei + ti))
+        second.append((er - tr, ei - ti))
+    return first + second
+
+
+def turned(re, im, k, count, sign):
+    if k == 0:
+        return re, im
+    if 4 * k == count:
+        return (-im, re) if sign > 0 else (im, -re)
+    cosine, sine = math.cos(2 * math.pi * k / count), sign * math.sin(2 * math.pi * k / count)
+    return cosine * re - sine * im, cosine * im + sine * re
+
+
+def odd_transform(values):
+    half = len(values) // 2
+    folded = [turned(values[s], -values[s + half], s, 4 * half, -1) for s in range(half)]
+    return complex_transform(folded, -1)
+
+
+def odd_inverse(modes):
+    half = len(modes)
+    folded = complex_transform(modes, 1)
+    first, second = [], []
+    for s, (re, im) in enumerate(folded):
+        re, im = turned(re, im, s, 4 * half, 1)
+        first.append(2.0 * re)
+        second.append(-2.0 * im)
+    return first + second
+
+
+def parity(shape, dim):
+    return lax.broadcasted_iota(jnp.int32, shape, dim) % 2 == 0
+
+
+def shifted(value, step, dim):
+    return pltpu.roll(value, step % value.shape[dim], dim)
+
+
+def pack_means(first, second, even_row, even_lane):
+    rows = []
+    for a, b in zip(first, second):
+        left = jnp.where(even_row, a, shifted(b, 1, 0))
+        right = jnp.where(even_row, shifted(a, -1, 0), b)
+        rows.append(left + right)
+    re, im = rows
+    left = jnp.where(even_lane, re, shifted(im, 1, 1))
+    right = jnp.where(even_lane, shifted(re, -1, 1), im)
+    return left + right
+
+
+def pack_cells(first, second, even_row, even_lane):
+    re = jnp.where(even_row, first[0], second[0])
+    im = jnp.where(even_row, first[1], second[1])
+    return jnp.where(even_lane, re, im)
+
+
+def unpack_cells(tile, even_row, even_lane):
+    found = []
+    for rows in (
+        jnp.where(even_row, tile, shifted(tile, 1, 0)),
+        jnp.where(even_row, shifted(tile, -1, 0), tile),
+    ):
+        re = jnp.where(even_lane, rows, shifted(rows, 1, 1))
+        im = jnp.where(even_lane, shifted(rows, -1, 1), rows)
+        found.append((re, im))
+    return found
+
+
+def neighbour_sum(below, here, above, weights):
+    along_first, masked, distance = weights
+    total = along_first[0] * above + along_first[1] * below
+    for dim in (0, 1):
+        upper, lower = masked[dim]
+        total = total + upper * shifted(here, -distance, dim)
+        total = total + lower * shifted(here, distance, dim)
+    return total
+
+
+def updated(forcing, inverse, columns, weights):
+    results, rest = [], []
+    for part in (0, 1):
+        below, here, above = (column[part] for column in columns)
+        rest.append(forcing[part] - neighbour_sum(below, here, above, weights))
+    a, b, c = inverse
+    r0, r1 = rest
+    results.append((1.0 - OMEGA) * columns[1][0] + (a * r0 + b * r1))
+    results.append((1.0 - OMEGA) * columns[1][1] + (c * r1 - b * r0))
+    return results
+
+
+HALO = 2
+
+
 def whole_kernel(groups, slabs, shift_table, residual_hbm, capacity_hbm, out_ref, *scratch):
-    (series, spectrum, returned, values, result) = scratch[:5]
-    residual_ref = scratch[-1]
-    scratch = scratch[:-1]
+    (
+        res, loc, far, seq, sendx, field, inverse0, vone, vtwo, coarse_out, gathered, back, edges,
+        result, merged, wave, gotb, outgoing, table,
+    ) = scratch[:19]
     depth = GRID_DEPTH
-    forcings = scratch[5 : 5 + depth]
-    caps = scratch[5 + depth : 5 + 2 * depth]
-    inverses = scratch[5 + 2 * depth : 5 + 3 * depth]
-    firsts = scratch[5 + 3 * depth : 5 + 4 * depth]
-    seconds = scratch[5 + 4 * depth : 5 + 5 * depth]
-    send1, recv1, send2, recv2, send3, recv3, send4, recv4, own, sendc, recvc, ready = scratch[
-        5 + 5 * depth :
-    ]
-    steps, thick = residual_ref.shape[:2]
-    planes = thick // groups
+    rest = scratch[19:]
+    forcings = (None,) + rest[: depth - 1]
+    rest = rest[depth - 1 :]
+    caps, rest = rest[:depth], rest[depth:]
+    inverses = (None,) + rest[: depth - 1]
+    rest = rest[depth - 1 :]
+    firsts = (None,) + rest[: depth - 1]
+    rest = rest[depth - 1 :]
+    seconds = (None,) + rest[: depth - 1]
+    rest = rest[depth - 1 :]
+    (
+        own, far_send, far_recv, loc_send, loc_recv, x_send, x_recv, d_send, d_recv, h_send, h_recv,
+        e_send, e_recv, g_send, g_recv, b_send, b_recv, r_send, r_recv, w_send, w_recv, o_send,
+        o_recv, c_send, c_recv, ready,
+    ) = rest
+    steps, thick = res.shape[:2]
+    half = thick // 2
+    slots = field.shape[1] // 2
+    wide = thick + 2 * HALO
     length = groups * steps
-    devices = groups * slabs
-    ratio_step = ALPHA_CORNER ** (1.0 / length)
-    mine, slab = lax.axis_index("tm"), lax.axis_index("space")
-    me = mine * slabs + slab
-    base = slab * thick + mine * planes
-
-    def peer_of(k):
-        to_tm = lax.rem(mine + k, groups)
-        to_space = lax.rem(slab + k // groups, slabs)
-        return to_tm * slabs + to_space, to_tm, to_space
-
-    own_slab = pl.ds(slab * thick, thick)
-    take_residual = pltpu.make_async_copy(residual_hbm, residual_ref, own.at[3 * planes])
-    take_capacity = pltpu.make_async_copy(
-        capacity_hbm, caps[0].at[own_slab], own.at[3 * planes + 1]
-    )
-    take_residual.start()
+    rate = ALPHA_CORNER ** (1.0 / length)
+    tile = res.shape[-2:]
+    m, s = lax.axis_index("tm"), lax.axis_index("space")
+    y, x = m // 2, lax.rem(m, 2)
+    z, c = s // 2, lax.rem(s, 2)
+    layers = slabs // 2
+    sig = lax.rem(y + z, 2)
+    slab = 2 * z + sig
+    keeper = sig == c
+    is_low, is_high = slab == 0, slab == slabs - 1
+
+    def at(ty, tx, tz, tc):
+        return (2 * ty + tx, 2 * tz + tc)
+
+    def plane_of(h, i):
+        return i if h == 0 else thick - 1 - i
+
+    def drain(ref, semaphore):
+        pltpu.make_async_copy(ref, ref, semaphore).wait()
+
+    def send(source, target, send_sem, recv_sem, device):
+        pltpu.make_async_remote_copy(
+            src_ref=source,
+            dst_ref=target,
+            send_sem=send_sem,
+            recv_sem=recv_sem,
+            device_id=device,
+            device_id_type=MESH,
+        ).start()
+
+    takes = []
+    for i in range(half):
+        for h in (0, 1):
+            p = plane_of(h, i)
+            copy = pltpu.make_async_copy(residual_hbm.at[:, p], res.at[:, p], own.at[p])
+            copy.start()
+            takes.append((p, copy))
+    own_slab = pl.ds(HALO + s * thick, thick)
+    take_capacity = pltpu.make_async_copy(capacity_hbm, caps[0].at[own_slab], own.at[thick])
     take_capacity.start()
+
     barrier = pltpu.get_barrier_semaphore()
-
-    partner = slab + 1 - 2 * lax.rem(slab, 2)
-    below, above = slab >= 2, slab < slabs - 2
+    below, above = z > 0, z < layers - 1
     sides = jnp.where(below, 1, 0) + jnp.where(above, 1, 0)
 
-    def tell_sides(semaphore):
-        for there, step in ((below, -2), (above, 2)):
-
-            @pl.when(there)
-            def _():
-                pl.semaphore_signal(
-                    semaphore, inc=1, device_id=(mine, slab + step), device_id_type=MESH
-                )
-
-    for d in range(1, groups):
-        pl.semaphore_signal(
-            barrier, inc=1, device_id=(lax.rem(mine + d, groups), slab), device_id_type=MESH
-        )
-    tell_sides(barrier)
-    pl.semaphore_signal(barrier, inc=1, device_id=(mine, partner), device_id_type=MESH)
-    for level in range(depth):
+    def greet(device):
+        pl.semaphore_signal(barrier, inc=1, device_id=device, device_id_type=MESH)
+
+    greet(at(1 - y, x, z, 0))
+    greet(at(1 - y, x, z, 1))
+    for there, dz in ((below, -1), (above, 1)):
+
+        @pl.when(there)
+        def _():
+            greet(at(y, x, z + dz, 0))
+            greet(at(y, x, z + dz, 1))
+
+    greet(at(y, 1 - x, z, c))
+    greet(at(y, x, z, 1 - c))
+
+    for level in range(1, depth):
         for buffer in (firsts[level], seconds[level]):
             empty = jnp.zeros(buffer.shape[1:], jnp.float32)
             buffer[0] = empty
             buffer[buffer.shape[0] - 1] = empty
-    take_residual.wait()
-    pl.semaphore_wait(barrier, groups + sides)
-
-    first_sends = []
-    for p in range(planes):
-        for d in range(1, groups):
-            to_tm = lax.rem(mine + d, groups)
-            copy = pltpu.make_async_remote_copy(
-                src_ref=residual_ref.at[:, to_tm * planes + p],
-                dst_ref=series.at[p, pl.ds(mine * steps, steps)],
-                send_sem=send1.at[p, d],
-                recv_sem=recv1.at[p, d],
-                device_id=(to_tm, slab),
-                device_id_type=MESH,
+    for k in range(shift_table.shape[0]):
+        for column in range(3):
+            table[k, column] = jnp.float32(shift_table[k, column])
+    caps[0][pl.ds(0, HALO)] = jnp.ones((HALO,) + tile, jnp.float32)
+    caps[0][pl.ds(HALO + slabs * thick, HALO)] = jnp.ones((HALO,) + tile, jnp.float32)
+
+    @pl.when(is_low)
+    def _():
+        for j in range(HALO):
+            field[j] = jnp.zeros(field.shape[1:], jnp.float32)
+        vtwo[0] = jnp.zeros(vtwo.shape[1:], jnp.float32)
+
+    @pl.when(is_high)
+    def _():
+        for j in range(HALO):
+            field[wide - 1 - j] = jnp.zeros(field.shape[1:], jnp.float32)
+        vtwo[wide - 1] = jnp.zeros(vtwo.shape[1:], jnp.float32)
+
+    pl.semaphore_wait(barrier, 4 + 2 * sides)
+
+    waited = {}
+    for p, copy in takes:
+        waited[p] = copy
+
+    for i in range(half):
+        for h in (0, 1):
+            waited[plane_of(h, i)].wait()
+
+        @pl.when(keeper)
+        def _():
+            for h in (0, 1):
+                p = plane_of(h, i)
+
+                @pl.when(c == h)
+                def _():
+                    pltpu.make_async_copy(res.at[:, p], loc.at[i], loc_recv.at[i]).start()
+
+                @pl.when(c != h)
+                def _():
+                    send(res.at[:, p], loc.at[i], loc_send.at[i], loc_recv.at[i], at(y, x, z, 1 - c))
+
+        @pl.when(jnp.logical_not(keeper))
+        def _():
+            for h in (0, 1):
+                p = plane_of(h, i)
+                send(
+                    res.at[:, p], far.at[i], far_send.at[i, h], far_recv.at[i], at(1 - y, x, z, h)
+                )
+
+    for turn in range(layers - 1):
+        for there, dz in ((below, -1), (above, 1)):
+
+            @pl.when(there)
+            def _():
+                pl.semaphore_signal(
+                    ready.at[turn], inc=1, device_id=at(y, x, z + dz, c), device_id_type=MESH
+                )
+
+        pl.semaphore_wait(ready.at[turn], sides)
+
+    take_capacity.wait()
+    for d in range(1, layers):
+        send(
+            caps[0].at[own_slab],
+            caps[0].at[own_slab],
+            c_send.at[d],
+            c_recv.at[d],
+            (m, lax.rem(s + 2 * d, slabs)),
+        )
+
+    def rows_from(d):
+        return pl.ds(HALO + lax.rem(s + slabs - 2 * d, slabs) * thick, thick)
+
+    def forward_cap(d):
+        rows = rows_from(d)
+        send(
+            caps[0].at[rows],
+            caps[0].at[rows],
+            c_send.at[layers + d],
+            c_recv.at[layers + d],
+            at(y, x, z, 1 - c),
+        )
+
+    forward_cap(0)
+
+    def power(ty):
+        exponent = [rate ** (a * length // 2 + b * steps) for a in (0, 1) for b in (0, 1)]
+        low = jnp.where(x == 0, jnp.float32(exponent[0]), jnp.float32(exponent[1]))
+        high = jnp.where(x == 0, jnp.float32(exponent[2]), jnp.float32(exponent[3]))
+        return jnp.where(ty == 0, low, high)
+
+    here_power, there_power = power(y), power(1 - y)
+    sign = jnp.where(y == 0, 1.0, -1.0).astype(jnp.float32)
+    first_x = x == 0
+    keep_own = jnp.where(first_x, here_power, sign * here_power)
+    keep_far = jnp.where(first_x, there_power, -sign * there_power)
+    give_own = jnp.where(first_x, sign * here_power, here_power)
+    give_far = jnp.where(first_x, -sign * there_power, there_power)
+
+    def combine(i):
+        drain(loc.at[i], loc_recv.at[i])
+        drain(far.at[i], far_recv.at[i])
+        for t in range(steps):
+            a, b = loc[i, t] * (rate**t), far[i, t] * (rate**t)
+            sendx[i, t] = give_own * a + give_far * b
+        send(
+            sendx.at[i],
+            seq.at[i, pl.ds(x * steps, steps)],
+            x_send.at[i],
+            x_recv.at[i],
+            at(y, 1 - x, z, c),
+        )
+        for t in range(steps):
+            a, b = loc[i, t] * (rate**t), far[i, t] * (rate**t)
+            seq[i, x * steps + t] = keep_own * a + keep_far * b
+
+    in_layer = c != sig
+    halo_y = jnp.where(in_layer, 1 - y, y)
+    halo_z = jnp.where(in_layer, z, z + 2 * c - 1)
+    halo_there = jnp.logical_or(in_layer, jnp.logical_and(halo_z >= 0, halo_z < layers))
+
+    def transform(i):
+        drain(sendx.at[i], x_recv.at[i])
+        plane = jnp.where(c == 0, i, thick - 1 - i) + HALO
+
+        @pl.when(x == 0)
+        def _():
+            modes = real_transform([seq[i, t] for t in range(2 * steps)])
+            field[plane, 0, 0] = modes[0][0]
+            field[plane, 0, 1] = modes[steps][0]
+            for k in range(1, steps):
+                field[plane, k, 0] = modes[k][0]
+                field[plane, k, 1] = modes[k][1]
+
+        @pl.when(x == 1)
+        def _():
+            modes = odd_transform([seq[i, t] for t in range(2 * steps)])
+            for k in range(steps):
+                field[plane, k, 0] = modes[k][0]
+                field[plane, k, 1] = modes[k][1]
+
+        given = field.at[plane, pl.ds((1 - c) * slots, slots)]
+        send(given, given, d_send.at[i], d_recv.at[i], at(y, x, z, 1 - c))
+        if i < HALO:
+            target = plane + thick * (1 - 2 * c)
+
+            @pl.when(halo_there)
+            def _():
+                for k in (0, 1):
+                    part = pl.ds(k * slots, slots)
+                    send(
+                        field.at[plane, part],
+                        field.at[target, part],
+                        h_send.at[i, k],
+                        h_recv.at[1 - c, i],
+                        at(halo_y, x, halo_z, k),
+                    )
+
+    def shifts_of(slot):
+        return tuple(table[slot, column] for column in range(3))
+
+    def coarse_tables():
+        for d in range(1, layers):
+            drain(caps[0].at[rows_from(d)], c_recv.at[d])
+            forward_cap(d)
+        for d in range(layers):
+            drain(caps[0].at[own_slab], c_recv.at[layers + d])
+        solver_shifts = shifts_of(x * 2 * slots + c * slots + slab)
+        cells = caps[0][pl.ds(HALO, slabs * thick)]
+        caps[1][...] = block_mean(cells, 1)
+        for level in range(1, depth):
+            prepare_level(level, caps, inverses, solver_shifts)
+
+    spread0, unused = level_coefficients(0)
+
+    def fine_tables():
+        inside = [jnp.float32(1.0)] * wide
+        for j in range(HALO):
+            inside[j] = jnp.where(is_low, 0.0, 1.0).astype(jnp.float32)
+            inside[wide - 1 - j] = jnp.where(is_high, 0.0, 1.0).astype(jnp.float32)
+
+        def body(f, carry):
+            s1, s2, s3 = shifts_of(x * 2 * slots + c * slots + f)
+            for j in range(wide):
+                cap = caps[0][slab * thick + j]
+                top, coupling = cap * s1 + 6.0 * spread0, cap * s2
+                bottom = cap * s3 + 6.0 * spread0
+                scale = (OMEGA * inside[j]) / (top * bottom + coupling * coupling)
+                inverse0[f, j, 0] = bottom * scale
+                inverse0[f, j, 1] = coupling * scale
+                inverse0[f, j, 2] = top * scale
+            return carry
+
+        lax.fori_loop(0, slots, body, 0)
+
+    combine(0)
+    combine(1)
+    coarse_tables()
+    combine(2)
+    transform(0)
+    fine_tables()
+    combine(3)
+    for i in range(1, half):
+        transform(i)
+
+    even_row, even_lane = parity(tile, 0), parity(tile, 1)
+    weights = neighbour_weights(0, tile)
+
+    def slot_at(i):
+        total, unit, rest_g, rest_i = 0, 1, slab, i
+        while unit < slots:
+            bit = lax.rem(lax.rem(rest_g, 2) + lax.rem(rest_i, 2), 2)
+            total = total + unit * bit
+            rest_g, rest_i = rest_g // 2, rest_i // 2
+            unit *= 2
+        return total
+
+    def member(g):
+        gz, gs = g // 2, lax.rem(g, 2)
+        return at(lax.rem(gs + gz, 2), x, gz, c)
+
+    for i in range(half):
+        drain(field.at[0, pl.ds(0, slots)], d_recv.at[i])
+    for side, there in ((0, jnp.logical_not(is_low)), (1, jnp.logical_not(is_high))):
+
+        @pl.when(there)
+        def _():
+            for i in range(HALO):
+                drain(field.at[0, pl.ds(0, slots)], h_recv.at[side, i])
+
+    def down(i, carry):
+        f = slot_at(slots - 1 - i)
+        q = c * slots + f
+        s1, s2, s3 = shifts_of(x * 2 * slots + q)
+        for j in range(wide):
+            re, im = field[j, q, 0], field[j, q, 1]
+            a, b, d = (inverse0[f, j, k] for k in range(3))
+            vone[j, 0] = a * re + b * im
+            vone[j, 1] = d * im - b * re
+        for j in range(1, wide - 1):
+            columns = [(vone[k, 0], vone[k, 1]) for k in (j - 1, j, j + 1)]
+            parts = updated(
+                (field[j, q, 0], field[j, q, 1]),
+                [inverse0[f, j, k] for k in range(3)],
+                columns,
+                weights,
             )
-            copy.start()
-            first_sends.append(copy)
-    own_steps = []
-    for p in range(planes):
-        copy = pltpu.make_async_copy(
-            residual_ref.at[:, mine * planes + p],
-            series.at[p, pl.ds(mine * steps, steps)],
-            own.at[p],
+            vtwo[j, f, 0] = parts[0]
+            vtwo[j, f, 1] = parts[1]
+        for pair in range(thick // 4):
+            packed = []
+            for plane in (0, 1):
+                sums = [0.0, 0.0]
+                for k in (0, 1):
+                    j = HALO + 4 * pair + 2 * plane + k
+                    cap = caps[0][slab * thick + j]
+                    near = [(vtwo[n, f, 0], vtwo[n, f, 1]) for n in (j - 1, j, j + 1)]
+                    re, im = near[1]
+                    turn = (s1 * re - s2 * im, s2 * re + s3 * im)
+                    for part in (0, 1):
+                        total = field[j, q, part] - neighbour_sum(
+                            near[0][part], near[1][part], near[2][part], weights
+                        )
+                        total = total - (6.0 * spread0 * near[1][part] + cap * turn[part])
+                        sums[part] = sums[part] + total
+                packed.append(sums)
+            coarse_out[f, pair] = 0.125 * pack_means(packed[0], packed[1], even_row, even_lane)
+
+        tiles = pl.ds(slab * (thick // 4), thick // 4)
+
+        @pl.when(f != slab)
+        def _():
+            send(coarse_out.at[f], gathered.at[tiles], g_send, g_recv, member(f))
+
+        @pl.when(f == slab)
+        def _():
+            for pair in range(thick // 4):
+                gathered[slab * (thick // 4) + pair] = coarse_out[f, pair]
+
+        return carry
+
+    lax.fori_loop(0, slots, down, 0)
+
+    low_y, low_z = jnp.where(sig == 0, y, 1 - y), jnp.where(sig == 0, z - 1, z)
+    high_y, high_z = jnp.where(sig == 0, 1 - y, y), jnp.where(sig == 0, z, z + 1)
+
+    @pl.when(jnp.logical_not(is_low))
+    def _():
+        send(
+            vtwo.at[HALO + 1], vtwo.at[wide - 1], e_send.at[0], e_recv.at[1], at(low_y, x, low_z, c)
         )
-        copy.start()
-        own_steps.append(copy)
-
-    for turn in range(slabs // 2 - 1):
-        tell_sides(ready.at[turn])
-        pl.semaphore_wait(ready.at[turn], sides)
-    last = slabs // 2 - 1
-    pl.semaphore_signal(ready.at[last], inc=1, device_id=(mine, partner), device_id_type=MESH)
-    pl.semaphore_wait(ready.at[last], 1)
-
-    take_capacity.wait()
-    cap_sends = []
-    for d in range(1, slabs // 2):
-        copy = pltpu.make_async_remote_copy(
-            src_ref=caps[0].at[own_slab],
-            dst_ref=caps[0].at[own_slab],
-            send_sem=sendc.at[d],
-            recv_sem=recvc.at[d],
-            device_id=(mine, lax.rem(slab + 2 * d, slabs)),
-            device_id_type=MESH,
+
+    @pl.when(jnp.logical_not(is_high))
+    def _():
+        send(
+            vtwo.at[wide - HALO - 2], vtwo.at[0], e_send.at[1], e_recv.at[0],
+            at(high_y, x, high_z, c),
         )
-        copy.start()
-        cap_sends.append(copy)
-
-    def forward_cap(d):
-        index = lax.rem(slab + slabs - 2 * d, slabs)
-        rows = pl.ds(index * thick, thick)
-        copy = pltpu.make_async_remote_copy(
-            src_ref=caps[0].at[rows],
-            dst_ref=caps[0].at[rows],
-            send_sem=sendc.at[slabs // 2 + d],
-            recv_sem=recvc.at[slabs // 2 + d],
-            device_id=(mine, partner),
-            device_id_type=MESH,
+
+    others = gathered.at[pl.ds(0, (slabs - 1) * (thick // 4))]
+    drain(others, g_recv)
+    for j in range(slabs * thick // 4):
+        first, second = unpack_cells(gathered[j], even_row, even_lane)
+        for k, parts in enumerate((first, second)):
+            forcings[1][2 * j + k, 0] = parts[0]
+            forcings[1][2 * j + k, 1] = parts[1]
+    solver_shifts = shifts_of(x * 2 * slots + c * slots + slab)
+    coarse = cycle(1, forcings, caps, inverses, firsts, seconds, solver_shifts, None)
+    for j in range(slabs * thick // 4 + 1):
+        back[j] = pack_cells(
+            (coarse[2 * j, 0], coarse[2 * j, 1]),
+            (coarse[2 * j + 1, 0], coarse[2 * j + 1, 1]),
+            even_row,
+            even_lane,
         )
-        copy.start()
-        return copy
-
-    cap_forwards = [forward_cap(0)]
-
-    def spread_mode(k, p):
-        peer, to_tm, to_space = peer_of(k)
-        return pltpu.make_async_remote_copy(
-            src_ref=spectrum.at[p, peer],
-            dst_ref=forcings[0].at[base + p],
-            send_sem=send2.at[p],
-            recv_sem=recv2.at[p],
-            device_id=(to_tm, to_space),
-            device_id_type=MESH,
+    span = thick // 4 + 1
+
+    def give(i, carry):
+        g = slot_at(slots - i)
+        send(
+            back.at[pl.ds(g * (thick // 4), span)], edges.at[slab], b_send, b_recv.at[slab],
+            member(g),
         )
-
-    own_modes = []
-    for p in range(planes):
-        own_steps[p].wait()
-        for d in range(1, groups):
-            first_sends[p * (groups - 1) + d - 1].wait_recv()
-        modes = real_transform([ratio_step**t * series[p, t] for t in range(length)])
-        spectrum[p, 0, 0] = modes[0][0]
-        spectrum[p, 0, 1] = modes[length // 2][0]
-        for k in range(1, length // 2):
-            spectrum[p, k, 0] = modes[k][0]
-            spectrum[p, k, 1] = modes[k][1]
-
-        def start_mode(k, carry):
-            spread_mode(k, p).start()
-            return carry
-
-        lax.fori_loop(1, devices, start_mode, 0)
-        copy = pltpu.make_async_copy(
-            spectrum.at[p, me], forcings[0].at[base + p], own.at[planes + p]
+        return carry
+
+    lax.fori_loop(1, slots, give, 0)
+    for k in range(span):
+        edges[slab, k] = back[slab * (thick // 4) + k]
+
+    for side, there in ((0, jnp.logical_not(is_low)), (1, jnp.logical_not(is_high))):
+
+        @pl.when(there)
+        def _():
+            drain(vtwo.at[0], e_recv.at[side])
+            drain(vtwo.at[0], e_send.at[side])
+
+    def up(i, carry):
+        f = slot_at(i)
+        q = c * slots + f
+
+        @pl.when(i > 0)
+        def _():
+            drain(edges.at[0], b_recv.at[f])
+
+        for k in range(span):
+            for n, extra in enumerate(unpack_cells(edges[f, k], even_row, even_lane)):
+                for j in (4 * k + 2 * n, 4 * k + 2 * n + 1):
+                    for part in (0, 1):
+                        vone[j, part] = vtwo[j, f, part] + extra[part]
+        for j in range(1, wide - 1):
+            columns = [(vone[k, 0], vone[k, 1]) for k in (j - 1, j, j + 1)]
+            parts = updated(
+                (field[j, q, 0], field[j, q, 1]),
+                [inverse0[f, j, k] for k in range(3)],
+                columns,
+                weights,
+            )
+            vtwo[j, f, 0] = parts[0]
+            vtwo[j, f, 1] = parts[1]
+        for j in range(HALO, wide - HALO):
+            columns = [(vtwo[k, f, 0], vtwo[k, f, 1]) for k in (j - 1, j, j + 1)]
+            parts = updated(
+                (field[j, q, 0], field[j, q, 1]),
+                [inverse0[f, j, k] for k in range(3)],
+                columns,
+                weights,
+            )
+            result[f, j - HALO, 0] = parts[0]
+            result[f, j - HALO, 1] = parts[1]
+        send(
+            result.at[f, pl.ds((1 - c) * half, half)], merged.at[q], r_send, r_recv,
+            at(y, x, z, 1 - c),
         )
-        copy.start()
-        own_modes.append(copy)
-
-    for d in range(1, slabs // 2):
-        cap_sends[d - 1].wait_recv()
-        cap_forwards.append(forward_cap(d))
-    for copy in cap_forwards:
-        copy.wait_recv()
-    shifts = []
-    for column in range(3):
-        value = jnp.float32(shift_table[0, column])
-        for k in range(1, devices):
-            value = jnp.where(me == k, jnp.float32(shift_table[k, column]), value)
-        shifts.append(value)
-    for level in range(depth):
-        prepare_level(level, caps, inverses, shifts)
-
-    def all_but_one(array, semaphore):
-        part = array.at[pl.ds(0, devices - 1)]
-        return pltpu.make_async_copy(part, part, semaphore)
-
-    for p in range(planes):
-        own_modes[p].wait()
-        all_but_one(forcings[0], recv2.at[p]).wait()
-
-    cycle(0, forcings, caps, inverses, firsts, seconds, shifts, result)
-
-    def send_back(k, p):
-        peer, to_tm, to_space = peer_of(k)
-        return pltpu.make_async_remote_copy(
-            src_ref=result.at[to_space * thick + to_tm * planes + p],
-            dst_ref=returned.at[p, me],
-            send_sem=send3.at[p],
-            recv_sem=recv3.at[p],
-            device_id=(to_tm, to_space),
-            device_id_type=MESH,
+        for k in range(half):
+            merged[q, k] = result[f, c * half + k]
+        return carry
+
+    lax.fori_loop(0, slots, up, 0)
+    drain(merged.at[pl.ds(0, slots)], r_recv)
+
+    def invert(i):
+        @pl.when(x == 0)
+        def _():
+            modes = [(merged[0, i, 0], None)]
+            modes += [(merged[k, i, 0], merged[k, i, 1]) for k in range(1, steps)]
+            modes += [(merged[0, i, 1], None)]
+            for t, value in enumerate(real_inverse(modes)):
+                wave[i, t] = value
+
+        @pl.when(x == 1)
+        def _():
+            modes = [(merged[k, i, 0], merged[k, i, 1]) for k in range(steps)]
+            for t, value in enumerate(odd_inverse(modes)):
+                wave[i, t] = value
+
+        send(
+            wave.at[i, pl.ds((1 - x) * steps, steps)], gotb.at[i], w_send.at[i], w_recv.at[i],
+            at(y, 1 - x, z, c),
         )
 
-    own_back = []
-    for p in range(planes):
-
-        def start_back(k, carry):
-            send_back(k, p).start()
-            return carry
-
-        lax.fori_loop(1, devices, start_back, 0)
-        copy = pltpu.make_async_copy(
-            result.at[base + p], returned.at[p, me], own.at[2 * planes + p]
+    inverse_here = 1.0 / (here_power * length)
+    inverse_there = 1.0 / (there_power * length)
+    own_sign = jnp.where(first_x, 1.0, sign).astype(jnp.float32)
+    got_sign = jnp.where(first_x, sign, 1.0).astype(jnp.float32)
+    far_own = jnp.where(first_x, 1.0, -sign).astype(jnp.float32)
+    far_got = jnp.where(first_x, -sign, 1.0).astype(jnp.float32)
+
+    def finish(i):
+        drain(gotb.at[i], w_recv.at[i])
+        p = c * half + i
+        for t in range(steps):
+            mine = wave[i, x * steps + t] * (rate**-t)
+            got = gotb[i, t] * (rate**-t)
+            outgoing[i, 1, t] = (far_own * inverse_there) * mine + (far_got * inverse_there) * got
+        send(
+            outgoing.at[i, 1], out_ref.at[:, p], o_send.at[i, 1], o_recv.at[c, i],
+            at(1 - y, x, z, sig),
         )
-        copy.start()
-        own_back.append(copy)
-
-    last_copies = []
-    for p in range(planes):
-        own_back[p].wait()
-        all_but_one(returned.at[p], recv3.at[p]).wait()
-        modes = [(returned[p, 0, 0], None)]
-        modes += [(returned[p, k, 0], returned[p, k, 1]) for k in range(1, length // 2)]
-        modes += [(returned[p, 0, 1], None)]
-        for t, value in enumerate(real_inverse(modes)):
-            values[p, t] = value * (ratio_step**-t / length)
-        for d in range(1, groups):
-            to_tm = lax.rem(mine + d, groups)
-            copy = pltpu.make_async_remote_copy(
-                src_ref=values.at[p, pl.ds(to_tm * steps, steps)],
-                dst_ref=out_ref.at[:, mine * planes + p],
-                send_sem=send4.at[p, d],
-                recv_sem=recv4.at[p, d],
-                device_id=(to_tm, slab),
-                device_id_type=MESH,
+        for t in range(steps):
+            mine = wave[i, x * steps + t] * (rate**-t)
+            got = gotb[i, t] * (rate**-t)
+            outgoing[i, 0, t] = (own_sign * inverse_here) * mine + (got_sign * inverse_here) * got
+
+        @pl.when(keeper)
+        def _():
+            for t in range(steps):
+                out_ref[t, p] = outgoing[i, 0, t]
+
+        @pl.when(jnp.logical_not(keeper))
+        def _():
+            send(
+                outgoing.at[i, 0], out_ref.at[:, p], o_send.at[i, 0], o_recv.at[c, i],
+                at(y, x, z, 1 - c),
             )
-            copy.start()
-            last_copies.append(copy)
-        out_ref[:, mine * planes + p] = values[p, pl.ds(mine * steps, steps)]
-
-    for copy in last_copies:
-        copy.wait()
-    for copy in first_sends + cap_sends + cap_forwards:
-        copy.wait_send()
-    for p in range(planes):
-        all_but_one(spectrum.at[p], send2.at[p]).wait()
-        all_but_one(result, send3.at[p]).wait()
+
+    for i in range(half):
+        invert(i)
+        if i > 0:
+            finish(i - 1)
+    finish(half - 1)
+
+    block = loc.at[0]
+    for i in range(half):
+
+        @pl.when(keeper)
+        def _():
+            drain(block, o_recv.at[1 - c, i])
+            drain(block, loc_send.at[i])
+
+        @pl.when(jnp.logical_not(keeper))
+        def _():
+            for h in (0, 1):
+                drain(block, o_recv.at[h, i])
+                drain(block, far_send.at[i, h])
+            drain(block, o_send.at[i, 0])
+
+        drain(block, o_send.at[i, 1])
+        drain(block, x_send.at[i])
+        drain(block, w_send.at[i])
+        drain(field.at[0, pl.ds(0, slots)], d_send.at[i])
+        if i < HALO:
+
+            @pl.when(halo_there)
+            def _():
+                for k in (0, 1):
+                    drain(field.at[0, pl.ds(0, slots)], h_send.at[i, k])
+
+    drain(others, g_send)
+    drain(edges.at[pl.ds(0, slots - 1)], b_send)
+    drain(merged.at[pl.ds(0, slots)], r_send)
+    for d in range(1, layers):
+        drain(caps[0].at[own_slab], c_send.at[d])
+    for d in range(layers):
+        drain(caps[0].at[own_slab], c_send.at[layers + d])
 
 
 def level_extents(extent):
@@ -700,11 +1131,13 @@
 
 def fused(groups, slabs, residual, capacity):
     steps, thick, second, third = residual.shape
-    length, devices = groups * steps, groups * slabs
-    planes, extent = thick // groups, slabs * thick
+    length = groups * steps
+    half, slots = thick // 2, steps // 2
+    extent, wide = slabs * thick, thick + 2 * HALO
     tile = (second, third)
     ratio_step = ALPHA_CORNER ** (1.0 / length)
-    angle = 2.0 * np.pi / length * np.arange(devices)
+    numbers = [2 * k for k in range(steps)] + [4 * k + 1 for k in range(steps)]
+    angle = 2.0 * np.pi / length * np.array(numbers)
     table = np.stack(
         [
             (1.0 - ratio_step * np.cos(angle)) / STEP_SIZE,
@@ -717,30 +1150,60 @@
     extents = level_extents(extent)
     vmem = lambda *shape: pltpu.VMEM(shape + tile, jnp.float32)
     sems = lambda *shape: pltpu.SemaphoreType.DMA(shape)
+    one = pltpu.SemaphoreType.DMA
+    layers, quarter = slabs // 2, thick // 4
     scratch = [
-        vmem(planes, length),
-        vmem(planes, devices, 2),
-        vmem(planes, devices, 2),
-        vmem(planes, length),
-        vmem(extent, 2),
-        *[vmem(n, 2) for n in extents],
-        *[vmem(n) for n in extents],
-        *[vmem(n, 3) for n in extents],
-        *[vmem(n + 2, 2) for n in extents],
-        *[vmem(n + 2, 2) for n in extents],
-        sems(planes, groups),
-        sems(planes, groups),
-        sems(planes),
-        sems(planes),
-        sems(planes),
-        sems(planes),
-        sems(planes, groups),
-        sems(planes, groups),
-        sems(3 * planes + 2),
-        sems(slabs),
-        sems(slabs),
-        pltpu.SemaphoreType.REGULAR((slabs // 2,)),
-        pltpu.VMEM(residual.shape, jnp.float32),
+        vmem(steps, thick),
+        vmem(half, steps),
+        vmem(half, steps),
+        vmem(half, 2 * steps),
+        vmem(half, steps),
+        vmem(wide, 2 * slots, 2),
+        vmem(slots, wide, 3),
+        vmem(wide, 2),
+        vmem(wide, slots, 2),
+        vmem(slots, quarter),
+        vmem(slabs * quarter),
+        vmem(slabs * quarter + 1),
+        vmem(slots, quarter + 1),
+        vmem(slots, thick, 2),
+        vmem(2 * slots, half, 2),
+        vmem(half, 2 * steps),
+        vmem(half, steps),
+        vmem(half, 2, steps),
+        pltpu.SMEM(table.shape, jnp.float32),
+        *[vmem(n, 2) for n in extents[1:]],
+        vmem(extent + 2 * HALO),
+        *[vmem(n) for n in extents[1:]],
+        *[vmem(n, 3) for n in extents[1:]],
+        *[vmem(n + 2, 2) for n in extents[1:]],
+        *[vmem(n + 2, 2) for n in extents[1:]],
+        sems(thick + 1),
+        sems(half, 2),
+        sems(half),
+        sems(half),
+        sems(half),
+        sems(half),
+        sems(half),
+        sems(half),
+        sems(half),
+        sems(HALO, 2),
+        sems(2, HALO),
+        sems(2),
+        sems(2),
+        one,
+        one,
+        one,
+        sems(slots),
+        one,
+        one,
+        sems(half),
+        sems(half),
+        sems(half, 2),
+        sems(2, half),
+        sems(2 * layers),
+        sems(2 * layers),
+        pltpu.SemaphoreType.REGULAR((layers - 1,)),
     ]
     return pl.pallas_call(
         functools.partial(whole_kernel, groups, slabs, table),
@@ -763,9 +1226,10 @@
     power = length & (length - 1) == 0
     return (
         power
-        and groups * slabs == length // 2
+        and groups == 4
         and slabs % 2 == 0
-        and thick % groups == 0
+        and slabs == length // 8
+        and thick == 8
         and all(n % 2 == 0 and n % min(n, BLOCK) == 0 for n in level_extents(slabs * thick))
         and (second, third) == (8, 128)
     )

time: 49.3 us -> 47.5 us (0.963)
  Pallas kernels: 46 us -> 44.7 us
    pallas_call x1, Pallas kernels: 46 us -> 44.7 us  [fused(): pl.pallas_call(functools.partial(whole_kernel, groups, slabs, table), out...]
where the time goes in v1:
time: 47.5 us; the launch traced here: 47.3 us
  Pallas kernels  44.7 us (94%)
  local copies, waits for them, and re-layouts  2.59 us (5%)
    pallas_call x1, Pallas kernels, fused(): pl.pallas_call(functools.partial(whole_kernel, groups, slabs, table), out...  44.7 us
    unnamed x5, local copies, waits for them, and re-layouts  2.59 us

profile of v1, /device:TPU:1, one launch (start us, length us, event | category | flops | bytes accessed | tf_op | source)
XLA Modules:
  0.0 47.3 jit_solution(455442694474631868)
XLA Ops:
  0.0 0.0 copy-start
  0.0 1.0 %copy-done = f32[16,8,8,128]{3,2,1,0:T(8,128)S(1)} copy-done((f32[16,8,8,128]{3,2,1,0:T(8,128)S(1)}, f32[16,8,8,128]{3,2,1,0:T(8,128)}, u32[]{:S(2)}) %copy-start) | copy-done | bytes 524312
  1.0 0.0 copy-start.1
  1.0 0.8 %copy-done.1 = f32[8,8,128]{2,1,0:T(8,128)S(1)} copy-done((f32[8,8,128]{2,1,0:T(8,128)S(1)}, f32[8,8,128]{2,1,0:T(8,128)}, u32[]{:S(2)}) %copy-start.1) | copy-done | bytes 32792
  1.8 44.7 %shard_map.28 = f32[16,8,8,128]{3,2,1,0:T(8,128)S(1)} custom-call(f32[16,8,8,128]{3,2,1,0:T(8,128)S(1)} %copy-done, f32[8,8,128]{2,1,0:T(8,128)S(1)} %copy-done.1), custom_call_target="tpu_custom_call" | custom-call | tf_op jit(solution)/shard_map/pallas_call | solution.py:1208
  46.5 0.8 %copy.4 = f32[16,8,8,128]{3,2,1,0:T(8,128)} copy(f32[16,8,8,128]{3,2,1,0:T(8,128)S(1)} %shard_map.28) | data formatting | bytes 1048576
Async XLA Ops:
  0.0 1.0 %copy-start = (f32[16,8,8,128]{3,2,1,0:T(8,128)S(1)}, f32[16,8,8,128]{3,2,1,0:T(8,128)}, u32[]{:S(2)}) copy-start(f32[16,8,8,128]{3,2,1,0:T(8,128)} %residual_hbm.1) | copy-start | bytes 1572868
  1.0 0.8 %copy-start.1 = (f32[8,8,128]{2,1,0:T(8,128)S(1)}, f32[8,8,128]{2,1,0:T(8,128)}, u32[]{:S(2)}) copy-start(f32[8,8,128]{2,1,0:T(8,128)} %capacity_hbm.1) | copy-start | bytes 98308

commit v2 on v1

--- a/solution.py
+++ b/solution.py
@@ -325,136 +325,6 @@
     return along_first, masked, distance
 
 
-def neighbours(wide, weights):
-    along_first, masked, distance = weights
-    centre = wide[1:-1]
-    total = along_first[0] * wide[2:] + along_first[1] * wide[:-2]
-    for dim in (0, 1):
-        extent = centre.shape[dim + 1]
-        if distance >= extent:
-            continue
-        upper, lower = masked[dim]
-        total = total + upper[None] * pltpu.roll(centre, extent - distance, dim + 1)
-        total = total + lower[None] * pltpu.roll(centre, distance, dim + 1)
-    return total
-
-
-def blocks_of(extent, largest, body):
-    block = min(extent, largest)
-
-    def step(i, carry):
-        body(pl.multiple_of(i * block, block), block)
-        return carry
-
-    if extent == block:
-        body(0, block)
-    else:
-        lax.fori_loop(0, extent // block, step, 0)
-
-
-BLOCK = 64
-
-
-def prepare_level(level, caps, inverses, shifts):
-    spread, unused = level_coefficients(level)
-    s1, s2, s3 = shifts
-
-    def body(start, block):
-        cap = caps[level][pl.ds(start, block)]
-        top, coupling, bottom = cap * s1 + 6.0 * spread, cap * s2, cap * s3 + 6.0 * spread
-        scale = OMEGA / (top * bottom + coupling * coupling)
-        inverses[level][pl.ds(start, block), 0] = bottom * scale
-        inverses[level][pl.ds(start, block), 1] = coupling * scale
-        inverses[level][pl.ds(start, block), 2] = top * scale
-        if level + 1 < GRID_DEPTH:
-            half = block // 2
-            caps[level + 1][pl.ds(start // 2, half)] = block_mean(cap, 2**level)
-
-    blocks_of(caps[level].shape[0], BLOCK, body)
-
-
-def smooth_first(forcing, target, inverse):
-    def body(start, block):
-        here = pl.ds(start, block)
-        a, b, c = inverse[here, 0], inverse[here, 1], inverse[here, 2]
-        re, im = forcing[here, 0], forcing[here, 1]
-        there = pl.ds(start + 1, block)
-        target[there, 0] = a * re + b * im
-        target[there, 1] = c * im - b * re
-
-    blocks_of(forcing.shape[0], BLOCK, body)
-
-
-def smooth(forcing, source, target, inverse, weights, offset=1, coarse=None):
-    def body(start, block):
-        here = pl.ds(start, block)
-        wide_re = source[pl.ds(start, block + 2), 0]
-        wide_im = source[pl.ds(start, block + 2), 1]
-        r0 = forcing[here, 0] - neighbours(wide_re, weights)
-        r1 = forcing[here, 1] - neighbours(wide_im, weights)
-        a, b, c = inverse[here, 0], inverse[here, 1], inverse[here, 2]
-        there = pl.ds(start + offset, block)
-        target[there, 0] = (1.0 - OMEGA) * wide_re[1:-1] + (a * r0 + b * r1)
-        target[there, 1] = (1.0 - OMEGA) * wide_im[1:-1] + (c * r1 - b * r0)
-
-    blocks_of(forcing.shape[0], BLOCK, body)
-
-
-def restrict_residual(level, forcing, source, cap, shifts, weights, target):
-    spread, unused = level_coefficients(level)
-    s1, s2, s3 = shifts
-
-    def body(start, block):
-        here = pl.ds(start, block)
-        wide_re = source[pl.ds(start, block + 2), 0]
-        wide_im = source[pl.ds(start, block + 2), 1]
-        re, im = wide_re[1:-1], wide_im[1:-1]
-        field = cap[here]
-        r0 = forcing[here, 0] - neighbours(wide_re, weights)
-        r1 = forcing[here, 1] - neighbours(wide_im, weights)
-        r0 = r0 - (6.0 * spread * re + field * (s1 * re - s2 * im))
-        r1 = r1 - (6.0 * spread * im + field * (s2 * re + s3 * im))
-        half = pl.ds(start // 2, block // 2)
-        target[half, 0] = block_mean(r0, 2**level)
-        target[half, 1] = block_mean(r1, 2**level)
-
-    blocks_of(forcing.shape[0], BLOCK, body)
-
-
-def add_coarse(target, coarse):
-    def body(start, block):
-        half = block // 2
-        for part in (0, 1):
-            extra = coarse[pl.ds(start // 2 + 1, half), part]
-            spread = jnp.broadcast_to(extra[:, None], (half, 2) + extra.shape[1:])
-            there = pl.ds(start + 1, block)
-            target[there, part] = target[there, part] + spread.reshape((block,) + extra.shape[1:])
-
-    blocks_of(target.shape[0] - 2, BLOCK, body)
-
-
-def cycle(level, forcings, caps, inverses, firsts, seconds, shifts, result):
-    forcing, inverse = forcings[level], inverses[level]
-    here, other = firsts[level], seconds[level]
-    weights = neighbour_weights(level, forcing.shape[-2:])
-    coarsest = level == GRID_DEPTH - 1
-    smooth_first(forcing, here, inverse)
-    for repeat in range((COARSE_SWEEPS if coarsest else SMOOTH) - 1):
-        smooth(forcing, here, other, inverse, weights)
-        here, other = other, here
-    if coarsest:
-        return here
-    restrict_residual(level, forcing, here, caps[level], shifts, weights, forcings[level + 1])
-    coarse = cycle(level + 1, forcings, caps, inverses, firsts, seconds, shifts, None)
-    add_coarse(here, coarse)
-    for repeat in range(SMOOTH):
-        last = repeat == SMOOTH - 1 and result is not None
-        target = result if last else other
-        smooth(forcing, here, target, inverse, weights, offset=0 if last else 1)
-        here, other = target, here
-    return here
-
-
 def complex_transform(values, sign):
     count = len(values)
     if count == 1:
@@ -515,12 +385,6 @@
     return left + right
 
 
-def pack_cells(first, second, even_row, even_lane):
-    re = jnp.where(even_row, first[0], second[0])
-    im = jnp.where(even_row, first[1], second[1])
-    return jnp.where(even_lane, re, im)
-
-
 def unpack_cells(tile, even_row, even_lane):
     found = []
     for rows in (
@@ -555,29 +419,124 @@
     return results
 
 
+def compact_rest(forcing, values, weights, even_row):
+    along_first, masked, distance = weights
+    found = [[None, None] for here in forcing]
+    for part in (0, 1):
+        column = [value[part] for value in values]
+        ups = [shifted(v, -1, 0) for v in column]
+        downs = [shifted(v, 1, 0) for v in column]
+        for j, value in enumerate(column):
+            zero = jnp.zeros_like(value)
+            after = downs[j + 1] if j + 1 < len(column) else zero
+            before = ups[j - 1] if j > 0 else zero
+            total = along_first[0] * jnp.where(even_row, ups[j], after)
+            total = total + along_first[1] * jnp.where(even_row, before, downs[j])
+            for dim in (0, 1):
+                if distance < value.shape[dim]:
+                    upper, lower = masked[dim]
+                    total = total + upper * shifted(value, -distance, dim)
+                    total = total + lower * shifted(value, distance, dim)
+            found[j][part] = forcing[j][part] - total
+    return found
+
+
+def compact_sweep(forcing, values, table, weights, even_row):
+    found = []
+    for j, (r0, r1) in enumerate(compact_rest(forcing, values, weights, even_row)):
+        a, b, c = (table[j, k] for k in range(3))
+        re, im = values[j]
+        found.append(
+            (
+                (1.0 - OMEGA) * re + (a * r0 + b * r1),
+                (1.0 - OMEGA) * im + (c * r1 - b * r0),
+            )
+        )
+    return found
+
+
+def compact_restrict(values, distance, even_row):
+    found = []
+    for pair in zip(values[0::2], values[1::2]):
+        parts = []
+        for first, second in zip(*pair):
+            left = jnp.where(even_row, first, shifted(second, 1, 0))
+            total = left + jnp.where(even_row, shifted(first, -1, 0), second)
+            for dim in (0, 1):
+                place = lax.broadcasted_iota(jnp.int32, total.shape, dim)
+                upper, lower = shifted(total, -distance, dim), shifted(total, distance, dim)
+                total = total + jnp.where((place // distance) % 2 == 0, upper, lower)
+            parts.append(0.125 * total)
+        found.append(parts)
+    return found
+
+
+def compact_cycle(level, forcing, tables, shifts, even_row):
+    table = tables[level]
+    spread, unused = level_coefficients(level)
+    s1, s2, s3 = shifts
+    weights = neighbour_weights(level, forcing[0][0].shape)
+    values = []
+    for j, (re, im) in enumerate(forcing):
+        a, b, c = (table[j, k] for k in range(3))
+        values.append((a * re + b * im, c * im - b * re))
+    coarsest = level == GRID_DEPTH - 1
+    for repeat in range((COARSE_SWEEPS if coarsest else SMOOTH) - 1):
+        values = compact_sweep(forcing, values, table, weights, even_row)
+    if coarsest:
+        return values
+    rest = compact_rest(forcing, values, weights, even_row)
+    for j, (re, im) in enumerate(values):
+        cap = table[j, 3]
+        rest[j][0] = rest[j][0] - (6.0 * spread * re + cap * (s1 * re - s2 * im))
+        rest[j][1] = rest[j][1] - (6.0 * spread * im + cap * (s2 * re + s3 * im))
+    coarse = compact_cycle(
+        level + 1, compact_restrict(rest, 2**level, even_row), tables, shifts, even_row
+    )
+    for j, value in enumerate(coarse):
+        values[2 * j] = tuple(
+            old + jnp.where(even_row, v, shifted(v, 1, 0)) for old, v in zip(values[2 * j], value)
+        )
+        values[2 * j + 1] = tuple(
+            old + jnp.where(even_row, shifted(v, -1, 0), v)
+            for old, v in zip(values[2 * j + 1], value)
+        )
+    for repeat in range(SMOOTH):
+        values = compact_sweep(forcing, values, table, weights, even_row)
+    return values
+
+
+def compact_table(level, caps, table, shifts, even_row):
+    spread, unused = level_coefficients(level)
+    s1, s2, s3 = shifts
+    for j in range(table.shape[0]):
+        cap = jnp.where(even_row, caps[2 * j], caps[2 * j + 1])
+        top, coupling, bottom = cap * s1 + 6.0 * spread, cap * s2, cap * s3 + 6.0 * spread
+        scale = OMEGA / (top * bottom + coupling * coupling)
+        table[j, 0] = bottom * scale
+        table[j, 1] = coupling * scale
+        table[j, 2] = top * scale
+        table[j, 3] = cap
+
+
 HALO = 2
+TOGETHER = 2
+PARTS = 2
 
 
 def whole_kernel(groups, slabs, shift_table, residual_hbm, capacity_hbm, out_ref, *scratch):
     (
-        res, loc, far, seq, sendx, field, inverse0, vone, vtwo, coarse_out, gathered, back, edges,
-        result, merged, wave, gotb, outgoing, table,
+        res, loc, far, seq, sendx, field, inverse0, vtwo, coarse_out, gathered, back, edges,
+        result, merged, wave, gotb, outgoing, table, near_cap,
     ) = scratch[:19]
     depth = GRID_DEPTH
     rest = scratch[19:]
-    forcings = (None,) + rest[: depth - 1]
-    rest = rest[depth - 1 :]
     caps, rest = rest[:depth], rest[depth:]
-    inverses = (None,) + rest[: depth - 1]
-    rest = rest[depth - 1 :]
-    firsts = (None,) + rest[: depth - 1]
-    rest = rest[depth - 1 :]
-    seconds = (None,) + rest[: depth - 1]
-    rest = rest[depth - 1 :]
+    tables, rest = (None,) + rest[: depth - 1], rest[depth - 1 :]
     (
         own, far_send, far_recv, loc_send, loc_recv, x_send, x_recv, d_send, d_recv, h_send, h_recv,
         e_send, e_recv, g_send, g_recv, b_send, b_recv, r_send, r_recv, w_send, w_recv, o_send,
-        o_recv, c_send, c_recv, ready,
+        o_recv, c_send, c_recv, n_send, n_recv, ready,
     ) = rest
     steps, thick = res.shape[:2]
     half = thick // 2
@@ -593,6 +552,8 @@
     sig = lax.rem(y + z, 2)
     slab = 2 * z + sig
     keeper = sig == c
+    side = lax.rem(c + x, 2)
+    part_steps = steps // PARTS
     is_low, is_high = slab == 0, slab == slabs - 1
 
     def at(ty, tx, tz, tc):
@@ -621,9 +582,12 @@
             copy = pltpu.make_async_copy(residual_hbm.at[:, p], res.at[:, p], own.at[p])
             copy.start()
             takes.append((p, copy))
-    own_slab = pl.ds(HALO + s * thick, thick)
+    own_slab = pl.ds(s * thick, thick)
     take_capacity = pltpu.make_async_copy(capacity_hbm, caps[0].at[own_slab], own.at[thick])
     take_capacity.start()
+    near_slab = pl.ds((2 + c) * thick, thick)
+    take_near = pltpu.make_async_copy(capacity_hbm, near_cap.at[near_slab], own.at[thick + 1])
+    take_near.start()
 
     barrier = pltpu.get_barrier_semaphore()
     below, above = z > 0, z < layers - 1
@@ -641,19 +605,21 @@
             greet(at(y, x, z + dz, 0))
             greet(at(y, x, z + dz, 1))
 
-    greet(at(y, 1 - x, z, c))
+    greet(at(y, 1 - x, z, 1 - c))
     greet(at(y, x, z, 1 - c))
 
-    for level in range(1, depth):
-        for buffer in (firsts[level], seconds[level]):
-            empty = jnp.zeros(buffer.shape[1:], jnp.float32)
-            buffer[0] = empty
-            buffer[buffer.shape[0] - 1] = empty
     for k in range(shift_table.shape[0]):
         for column in range(3):
             table[k, column] = jnp.float32(shift_table[k, column])
-    caps[0][pl.ds(0, HALO)] = jnp.ones((HALO,) + tile, jnp.float32)
-    caps[0][pl.ds(HALO + slabs * thick, HALO)] = jnp.ones((HALO,) + tile, jnp.float32)
+    ones = jnp.ones((thick,) + tile, jnp.float32)
+
+    @pl.when(jnp.logical_not(below))
+    def _():
+        near_cap[pl.ds(thick, thick)] = ones
+
+    @pl.when(jnp.logical_not(above))
+    def _():
+        near_cap[pl.ds(4 * thick, thick)] = ones
 
     @pl.when(is_low)
     def _():
@@ -682,23 +648,43 @@
             for h in (0, 1):
                 p = plane_of(h, i)
 
-                @pl.when(c == h)
+                @pl.when(side == h)
                 def _():
                     pltpu.make_async_copy(res.at[:, p], loc.at[i], loc_recv.at[i]).start()
 
-                @pl.when(c != h)
+                @pl.when(side != h)
                 def _():
                     send(res.at[:, p], loc.at[i], loc_send.at[i], loc_recv.at[i], at(y, x, z, 1 - c))
 
         @pl.when(jnp.logical_not(keeper))
         def _():
-            for h in (0, 1):
-                p = plane_of(h, i)
-                send(
-                    res.at[:, p], far.at[i], far_send.at[i, h], far_recv.at[i], at(1 - y, x, z, h)
-                )
-
-    for turn in range(layers - 1):
+            for k in range(PARTS):
+                span = pl.ds(k * part_steps, part_steps)
+                for h in (0, 1):
+                    send(
+                        res.at[span, plane_of(h, i)], far.at[i, span], far_send.at[i, k, h],
+                        far_recv.at[i, k], at(1 - y, x, z, lax.rem(h + x, 2)),
+                    )
+
+    take_near.wait()
+    send(
+        near_cap.at[near_slab], near_cap.at[near_slab], n_send.at[2], n_recv.at[2],
+        at(y, x, z, 1 - c),
+    )
+    near_there = jnp.where(c == 0, below, above)
+
+    @pl.when(near_there)
+    def _():
+        for k in (0, 1):
+            send(
+                near_cap.at[near_slab],
+                near_cap.at[pl.ds((4 - 3 * c) * thick, thick)],
+                n_send.at[k],
+                n_recv.at[1 - c],
+                at(y, x, z + 2 * c - 1, k),
+            )
+
+    def tell_sides(turn):
         for there, dz in ((below, -1), (above, 1)):
 
             @pl.when(there)
@@ -707,20 +693,23 @@
                     ready.at[turn], inc=1, device_id=at(y, x, z + dz, c), device_id_type=MESH
                 )
 
+    def hear_sides(turn):
         pl.semaphore_wait(ready.at[turn], sides)
 
-    take_capacity.wait()
-    for d in range(1, layers):
-        send(
-            caps[0].at[own_slab],
-            caps[0].at[own_slab],
-            c_send.at[d],
-            c_recv.at[d],
-            (m, lax.rem(s + 2 * d, slabs)),
-        )
+    def share_capacity():
+        take_capacity.wait()
+        for d in range(1, layers):
+            send(
+                caps[0].at[own_slab],
+                caps[0].at[own_slab],
+                c_send.at[d],
+                c_recv.at[d],
+                (m, lax.rem(s + 2 * d, slabs)),
+            )
+        forward_cap(0)
 
     def rows_from(d):
-        return pl.ds(HALO + lax.rem(s + slabs - 2 * d, slabs) * thick, thick)
+        return pl.ds(lax.rem(s + slabs - 2 * d, slabs) * thick, thick)
 
     def forward_cap(d):
         rows = rows_from(d)
@@ -732,8 +721,6 @@
             at(y, x, z, 1 - c),
         )
 
-    forward_cap(0)
-
     def power(ty):
         exponent = [rate ** (a * length // 2 + b * steps) for a in (0, 1) for b in (0, 1)]
         low = jnp.where(x == 0, jnp.float32(exponent[0]), jnp.float32(exponent[1]))
@@ -750,29 +737,32 @@
 
     def combine(i):
         drain(loc.at[i], loc_recv.at[i])
-        drain(far.at[i], far_recv.at[i])
-        for t in range(steps):
-            a, b = loc[i, t] * (rate**t), far[i, t] * (rate**t)
-            sendx[i, t] = give_own * a + give_far * b
-        send(
-            sendx.at[i],
-            seq.at[i, pl.ds(x * steps, steps)],
-            x_send.at[i],
-            x_recv.at[i],
-            at(y, 1 - x, z, c),
-        )
-        for t in range(steps):
-            a, b = loc[i, t] * (rate**t), far[i, t] * (rate**t)
-            seq[i, x * steps + t] = keep_own * a + keep_far * b
-
-    in_layer = c != sig
+        for k in range(PARTS):
+            span = pl.ds(k * part_steps, part_steps)
+            drain(far.at[i, span], far_recv.at[i, k])
+            for t in range(k * part_steps, (k + 1) * part_steps):
+                a, b = loc[i, t] * (rate**t), far[i, t] * (rate**t)
+                sendx[i, t] = give_own * a + give_far * b
+            send(
+                sendx.at[i, span],
+                seq.at[i, pl.ds(x * steps + k * part_steps, part_steps)],
+                x_send.at[i, k],
+                x_recv.at[i, k],
+                at(y, 1 - x, z, 1 - c),
+            )
+            for t in range(k * part_steps, (k + 1) * part_steps):
+                a, b = loc[i, t] * (rate**t), far[i, t] * (rate**t)
+                seq[i, x * steps + t] = keep_own * a + keep_far * b
+
+    in_layer = side != sig
     halo_y = jnp.where(in_layer, 1 - y, y)
-    halo_z = jnp.where(in_layer, z, z + 2 * c - 1)
+    halo_z = jnp.where(in_layer, z, z + 2 * side - 1)
     halo_there = jnp.logical_or(in_layer, jnp.logical_and(halo_z >= 0, halo_z < layers))
 
     def transform(i):
-        drain(sendx.at[i], x_recv.at[i])
-        plane = jnp.where(c == 0, i, thick - 1 - i) + HALO
+        for k in range(PARTS):
+            drain(sendx.at[i, pl.ds(0, part_steps)], x_recv.at[i, k])
+        plane = jnp.where(side == 0, i, thick - 1 - i) + HALO
 
         @pl.when(x == 0)
         def _():
@@ -793,7 +783,7 @@
         given = field.at[plane, pl.ds((1 - c) * slots, slots)]
         send(given, given, d_send.at[i], d_recv.at[i], at(y, x, z, 1 - c))
         if i < HALO:
-            target = plane + thick * (1 - 2 * c)
+            target = plane + thick * (1 - 2 * side)
 
             @pl.when(halo_there)
             def _():
@@ -803,28 +793,43 @@
                         field.at[plane, part],
                         field.at[target, part],
                         h_send.at[i, k],
-                        h_recv.at[1 - c, i],
+                        h_recv.at[1 - side, i],
                         at(halo_y, x, halo_z, k),
                     )
 
     def shifts_of(slot):
         return tuple(table[slot, column] for column in range(3))
 
-    def coarse_tables():
+    even_row, even_lane = parity(tile, 0), parity(tile, 1)
+    solver_shifts = shifts_of(x * 2 * slots + c * slots + slab)
+
+    def pass_capacity():
         for d in range(1, layers):
             drain(caps[0].at[rows_from(d)], c_recv.at[d])
             forward_cap(d)
+
+    def coarse_tables():
         for d in range(layers):
             drain(caps[0].at[own_slab], c_recv.at[layers + d])
-        solver_shifts = shifts_of(x * 2 * slots + c * slots + slab)
-        cells = caps[0][pl.ds(HALO, slabs * thick)]
-        caps[1][...] = block_mean(cells, 1)
         for level in range(1, depth):
-            prepare_level(level, caps, inverses, solver_shifts)
+            caps[level][...] = block_mean(caps[level - 1][...], 2 ** (level - 1))
+            compact_table(level, caps[level], tables[level], solver_shifts, even_row)
 
     spread0, unused = level_coefficients(0)
 
+    cap_base = (2 + sig) * thick - HALO
+
     def fine_tables():
+        drain(near_cap.at[near_slab], n_recv.at[2])
+
+        @pl.when(below)
+        def _():
+            drain(near_cap.at[near_slab], n_recv.at[0])
+
+        @pl.when(above)
+        def _():
+            drain(near_cap.at[near_slab], n_recv.at[1])
+
         inside = [jnp.float32(1.0)] * wide
         for j in range(HALO):
             inside[j] = jnp.where(is_low, 0.0, 1.0).astype(jnp.float32)
@@ -833,7 +838,7 @@
         def body(f, carry):
             s1, s2, s3 = shifts_of(x * 2 * slots + c * slots + f)
             for j in range(wide):
-                cap = caps[0][slab * thick + j]
+                cap = near_cap[cap_base + j]
                 top, coupling = cap * s1 + 6.0 * spread0, cap * s2
                 bottom = cap * s3 + 6.0 * spread0
                 scale = (OMEGA * inside[j]) / (top * bottom + coupling * coupling)
@@ -844,17 +849,20 @@
 
         lax.fori_loop(0, slots, body, 0)
 
-    combine(0)
-    combine(1)
-    coarse_tables()
-    combine(2)
-    transform(0)
-    fine_tables()
-    combine(3)
-    for i in range(1, half):
+    for turn in range(layers - 1):
+        tell_sides(turn)
+        if turn > 0:
+            combine(turn - 1)
+        hear_sides(turn)
+    share_capacity()
+    for i in range(layers - 2, half):
+        combine(i)
+    for i in range(half):
         transform(i)
-
-    even_row, even_lane = parity(tile, 0), parity(tile, 1)
+        if i == 1:
+            fine_tables()
+    pass_capacity()
+
     weights = neighbour_weights(0, tile)
 
     def slot_at(i):
@@ -872,65 +880,75 @@
 
     for i in range(half):
         drain(field.at[0, pl.ds(0, slots)], d_recv.at[i])
-    for side, there in ((0, jnp.logical_not(is_low)), (1, jnp.logical_not(is_high))):
+    for end, there in ((0, jnp.logical_not(is_low)), (1, jnp.logical_not(is_high))):
 
         @pl.when(there)
         def _():
             for i in range(HALO):
-                drain(field.at[0, pl.ds(0, slots)], h_recv.at[side, i])
+                drain(field.at[0, pl.ds(0, slots)], h_recv.at[end, i])
+
+    def load_slot(f):
+        q = c * slots + f
+        forcing = [(field[j, q, 0], field[j, q, 1]) for j in range(wide)]
+        inverse = [[inverse0[f, j, k] for k in range(3)] for j in range(wide)]
+        return forcing, inverse
+
+    def residual_at(forcing, second, j, shifts):
+        s1, s2, s3 = shifts
+        cap = near_cap[cap_base + j]
+        re, im = second[j]
+        turn = (s1 * re - s2 * im, s2 * re + s3 * im)
+        found = []
+        for part in (0, 1):
+            total = forcing[j][part] - neighbour_sum(
+                *(second[n][part] for n in (j - 1, j, j + 1)), weights
+            )
+            found.append(total - (6.0 * spread0 * second[j][part] + cap * turn[part]))
+        return found
 
     def down(i, carry):
-        f = slot_at(slots - 1 - i)
-        q = c * slots + f
-        s1, s2, s3 = shifts_of(x * 2 * slots + q)
+        chosen = [slot_at(slots - 1 - TOGETHER * i - k) for k in range(TOGETHER)]
+        loaded = [load_slot(f) for f in chosen]
+        shifts = [shifts_of(x * 2 * slots + c * slots + f) for f in chosen]
+        first = [[] for f in chosen]
+        second = [[None] for f in chosen]
         for j in range(wide):
-            re, im = field[j, q, 0], field[j, q, 1]
-            a, b, d = (inverse0[f, j, k] for k in range(3))
-            vone[j, 0] = a * re + b * im
-            vone[j, 1] = d * im - b * re
+            for n, (forcing, inverse) in enumerate(loaded):
+                (re, im), (a, b, d) = forcing[j], inverse[j]
+                first[n].append((a * re + b * im, d * im - b * re))
         for j in range(1, wide - 1):
-            columns = [(vone[k, 0], vone[k, 1]) for k in (j - 1, j, j + 1)]
-            parts = updated(
-                (field[j, q, 0], field[j, q, 1]),
-                [inverse0[f, j, k] for k in range(3)],
-                columns,
-                weights,
-            )
-            vtwo[j, f, 0] = parts[0]
-            vtwo[j, f, 1] = parts[1]
+            for n, (forcing, inverse) in enumerate(loaded):
+                second[n].append(updated(forcing[j], inverse[j], first[n][j - 1 : j + 2], weights))
+                for part in (0, 1):
+                    vtwo[j, chosen[n], part] = second[n][j][part]
         for pair in range(thick // 4):
-            packed = []
+            packed = [[[None, None], [None, None]] for f in chosen]
             for plane in (0, 1):
-                sums = [0.0, 0.0]
                 for k in (0, 1):
-                    j = HALO + 4 * pair + 2 * plane + k
-                    cap = caps[0][slab * thick + j]
-                    near = [(vtwo[n, f, 0], vtwo[n, f, 1]) for n in (j - 1, j, j + 1)]
-                    re, im = near[1]
-                    turn = (s1 * re - s2 * im, s2 * re + s3 * im)
-                    for part in (0, 1):
-                        total = field[j, q, part] - neighbour_sum(
-                            near[0][part], near[1][part], near[2][part], weights
-                        )
-                        total = total - (6.0 * spread0 * near[1][part] + cap * turn[part])
-                        sums[part] = sums[part] + total
-                packed.append(sums)
-            coarse_out[f, pair] = 0.125 * pack_means(packed[0], packed[1], even_row, even_lane)
+                    for n, (forcing, inverse) in enumerate(loaded):
+                        j = HALO + 4 * pair + 2 * plane + k
+                        rest = residual_at(forcing, second[n], j, shifts[n])
+                        for part in (0, 1):
+                            sofar = packed[n][plane][part]
+                            packed[n][plane][part] = rest[part] if k == 0 else sofar + rest[part]
+            for n, f in enumerate(chosen):
+                coarse_out[f, pair] = 0.125 * pack_means(*packed[n], even_row, even_lane)
 
         tiles = pl.ds(slab * (thick // 4), thick // 4)
-
-        @pl.when(f != slab)
-        def _():
-            send(coarse_out.at[f], gathered.at[tiles], g_send, g_recv, member(f))
-
-        @pl.when(f == slab)
-        def _():
-            for pair in range(thick // 4):
-                gathered[slab * (thick // 4) + pair] = coarse_out[f, pair]
+        for f in chosen:
+
+            @pl.when(f != slab)
+            def _():
+                send(coarse_out.at[f], gathered.at[tiles], g_send, g_recv, member(f))
+
+            @pl.when(f == slab)
+            def _():
+                for pair in range(thick // 4):
+                    gathered[slab * (thick // 4) + pair] = coarse_out[f, pair]
 
         return carry
 
-    lax.fori_loop(0, slots, down, 0)
+    lax.fori_loop(0, slots // TOGETHER, down, 0)
 
     low_y, low_z = jnp.where(sig == 0, y, 1 - y), jnp.where(sig == 0, z - 1, z)
     high_y, high_z = jnp.where(sig == 0, 1 - y, y), jnp.where(sig == 0, z, z + 1)
@@ -948,21 +966,24 @@
             at(high_y, x, high_z, c),
         )
 
+    coarse_tables()
     others = gathered.at[pl.ds(0, (slabs - 1) * (thick // 4))]
     drain(others, g_recv)
-    for j in range(slabs * thick // 4):
-        first, second = unpack_cells(gathered[j], even_row, even_lane)
-        for k, parts in enumerate((first, second)):
-            forcings[1][2 * j + k, 0] = parts[0]
-            forcings[1][2 * j + k, 1] = parts[1]
-    solver_shifts = shifts_of(x * 2 * slots + c * slots + slab)
-    coarse = cycle(1, forcings, caps, inverses, firsts, seconds, solver_shifts, None)
-    for j in range(slabs * thick // 4 + 1):
-        back[j] = pack_cells(
-            (coarse[2 * j, 0], coarse[2 * j, 1]),
-            (coarse[2 * j + 1, 0], coarse[2 * j + 1, 1]),
+    tiles_in = slabs * thick // 4
+    unpacked = []
+    for j in range(tiles_in):
+        cells = gathered[j]
+        re = jnp.where(even_lane, cells, shifted(cells, 1, 1))
+        im = jnp.where(even_lane, shifted(cells, -1, 1), cells)
+        unpacked.append((re, im))
+    coarse = compact_cycle(1, unpacked, tables, solver_shifts, even_row)
+    packed_cells = [jnp.where(even_lane, re, im) for re, im in coarse]
+    empty = jnp.zeros(tile, jnp.float32)
+    for j in range(tiles_in + 1):
+        back[j] = jnp.where(
             even_row,
-            even_lane,
+            packed_cells[j] if j < tiles_in else empty,
+            packed_cells[j - 1] if j > 0 else empty,
         )
     span = thick // 4 + 1
 
@@ -978,55 +999,48 @@
     for k in range(span):
         edges[slab, k] = back[slab * (thick // 4) + k]
 
-    for side, there in ((0, jnp.logical_not(is_low)), (1, jnp.logical_not(is_high))):
+    for end, there in ((0, jnp.logical_not(is_low)), (1, jnp.logical_not(is_high))):
 
         @pl.when(there)
         def _():
-            drain(vtwo.at[0], e_recv.at[side])
-            drain(vtwo.at[0], e_send.at[side])
+            drain(vtwo.at[0], e_recv.at[end])
+            drain(vtwo.at[0], e_send.at[end])
 
     def up(i, carry):
-        f = slot_at(i)
-        q = c * slots + f
-
-        @pl.when(i > 0)
-        def _():
-            drain(edges.at[0], b_recv.at[f])
-
+        chosen = [slot_at(TOGETHER * i + k) for k in range(TOGETHER)]
+        for k, f in enumerate(chosen):
+
+            @pl.when(TOGETHER * i + k > 0)
+            def _():
+                drain(edges.at[0], b_recv.at[f])
+
+        loaded = [load_slot(f) for f in chosen]
+        start = [[] for f in chosen]
+        third = [[None] for f in chosen]
         for k in range(span):
-            for n, extra in enumerate(unpack_cells(edges[f, k], even_row, even_lane)):
-                for j in (4 * k + 2 * n, 4 * k + 2 * n + 1):
-                    for part in (0, 1):
-                        vone[j, part] = vtwo[j, f, part] + extra[part]
+            for n, f in enumerate(chosen):
+                for u, extra in enumerate(unpack_cells(edges[f, k], even_row, even_lane)[::-1]):
+                    for j in (4 * k + 2 * u, 4 * k + 2 * u + 1):
+                        start[n].append([vtwo[j, f, part] + extra[part] for part in (0, 1)])
         for j in range(1, wide - 1):
-            columns = [(vone[k, 0], vone[k, 1]) for k in (j - 1, j, j + 1)]
-            parts = updated(
-                (field[j, q, 0], field[j, q, 1]),
-                [inverse0[f, j, k] for k in range(3)],
-                columns,
-                weights,
+            for n, (forcing, inverse) in enumerate(loaded):
+                third[n].append(updated(forcing[j], inverse[j], start[n][j - 1 : j + 2], weights))
+        for j in range(HALO, wide - HALO):
+            for n, (forcing, inverse) in enumerate(loaded):
+                parts = updated(forcing[j], inverse[j], third[n][j - 1 : j + 2], weights)
+                for part in (0, 1):
+                    result[chosen[n], j - HALO, part] = parts[part]
+        for f in chosen:
+            q = c * slots + f
+            send(
+                result.at[f, pl.ds((1 - side) * half, half)], merged.at[q], r_send, r_recv,
+                at(y, x, z, 1 - c),
             )
-            vtwo[j, f, 0] = parts[0]
-            vtwo[j, f, 1] = parts[1]
-        for j in range(HALO, wide - HALO):
-            columns = [(vtwo[k, f, 0], vtwo[k, f, 1]) for k in (j - 1, j, j + 1)]
-            parts = updated(
-                (field[j, q, 0], field[j, q, 1]),
-                [inverse0[f, j, k] for k in range(3)],
-                columns,
-                weights,
-            )
-            result[f, j - HALO, 0] = parts[0]
-            result[f, j - HALO, 1] = parts[1]
-        send(
-            result.at[f, pl.ds((1 - c) * half, half)], merged.at[q], r_send, r_recv,
-            at(y, x, z, 1 - c),
-        )
-        for k in range(half):
-            merged[q, k] = result[f, c * half + k]
+            for k in range(half):
+                merged[q, k] = result[f, side * half + k]
         return carry
 
-    lax.fori_loop(0, slots, up, 0)
+    lax.fori_loop(0, slots // TOGETHER, up, 0)
     drain(merged.at[pl.ds(0, slots)], r_recv)
 
     def invert(i):
@@ -1044,10 +1058,12 @@
             for t, value in enumerate(odd_inverse(modes)):
                 wave[i, t] = value
 
-        send(
-            wave.at[i, pl.ds((1 - x) * steps, steps)], gotb.at[i], w_send.at[i], w_recv.at[i],
-            at(y, 1 - x, z, c),
-        )
+        for k in range(PARTS):
+            send(
+                wave.at[i, pl.ds((1 - x) * steps + k * part_steps, part_steps)],
+                gotb.at[i, pl.ds(k * part_steps, part_steps)], w_send.at[i, k], w_recv.at[i, k],
+                at(y, 1 - x, z, 1 - c),
+            )
 
     inverse_here = 1.0 / (here_power * length)
     inverse_there = 1.0 / (there_power * length)
@@ -1056,58 +1072,68 @@
     far_own = jnp.where(first_x, 1.0, -sign).astype(jnp.float32)
     far_got = jnp.where(first_x, -sign, 1.0).astype(jnp.float32)
 
-    def finish(i):
-        drain(gotb.at[i], w_recv.at[i])
-        p = c * half + i
-        for t in range(steps):
+    def finish(i, k):
+        span = pl.ds(k * part_steps, part_steps)
+        drain(gotb.at[i, span], w_recv.at[i, k])
+        p = side * half + i
+        for t in range(k * part_steps, (k + 1) * part_steps):
             mine = wave[i, x * steps + t] * (rate**-t)
             got = gotb[i, t] * (rate**-t)
             outgoing[i, 1, t] = (far_own * inverse_there) * mine + (far_got * inverse_there) * got
         send(
-            outgoing.at[i, 1], out_ref.at[:, p], o_send.at[i, 1], o_recv.at[c, i],
-            at(1 - y, x, z, sig),
+            outgoing.at[i, 1, span], out_ref.at[span, p], o_send.at[i, k, 1],
+            o_recv.at[side, i, k], at(1 - y, x, z, sig),
         )
-        for t in range(steps):
+
+        def own_value(t):
             mine = wave[i, x * steps + t] * (rate**-t)
             got = gotb[i, t] * (rate**-t)
-            outgoing[i, 0, t] = (own_sign * inverse_here) * mine + (got_sign * inverse_here) * got
+            return (own_sign * inverse_here) * mine + (got_sign * inverse_here) * got
 
         @pl.when(keeper)
         def _():
-            for t in range(steps):
-                out_ref[t, p] = outgoing[i, 0, t]
+            for t in range(k * part_steps, (k + 1) * part_steps):
+                out_ref[t, p] = own_value(t)
 
         @pl.when(jnp.logical_not(keeper))
         def _():
+            for t in range(k * part_steps, (k + 1) * part_steps):
+                outgoing[i, 0, t] = own_value(t)
             send(
-                outgoing.at[i, 0], out_ref.at[:, p], o_send.at[i, 0], o_recv.at[c, i],
-                at(y, x, z, 1 - c),
+                outgoing.at[i, 0, span], out_ref.at[span, p], o_send.at[i, k, 0],
+                o_recv.at[side, i, k], at(y, x, z, 1 - c),
             )
 
     for i in range(half):
         invert(i)
-        if i > 0:
-            finish(i - 1)
-    finish(half - 1)
+    for i in range(half):
+        for k in range(PARTS):
+            finish(i, k)
 
     block = loc.at[0]
+    piece = loc.at[0, pl.ds(0, part_steps)]
     for i in range(half):
+        for k in range(PARTS):
+
+            @pl.when(keeper)
+            def _():
+                drain(piece, o_recv.at[1 - side, i, k])
+
+            @pl.when(jnp.logical_not(keeper))
+            def _():
+                for h in (0, 1):
+                    drain(piece, o_recv.at[h, i, k])
+                    drain(piece, far_send.at[i, k, h])
+                drain(piece, o_send.at[i, k, 0])
+
+            drain(piece, o_send.at[i, k, 1])
+            drain(piece, x_send.at[i, k])
+            drain(piece, w_send.at[i, k])
 
         @pl.when(keeper)
         def _():
-            drain(block, o_recv.at[1 - c, i])
             drain(block, loc_send.at[i])
 
-        @pl.when(jnp.logical_not(keeper))
-        def _():
-            for h in (0, 1):
-                drain(block, o_recv.at[h, i])
-                drain(block, far_send.at[i, h])
-            drain(block, o_send.at[i, 0])
-
-        drain(block, o_send.at[i, 1])
-        drain(block, x_send.at[i])
-        drain(block, w_send.at[i])
         drain(field.at[0, pl.ds(0, slots)], d_send.at[i])
         if i < HALO:
 
@@ -1119,6 +1145,13 @@
     drain(others, g_send)
     drain(edges.at[pl.ds(0, slots - 1)], b_send)
     drain(merged.at[pl.ds(0, slots)], r_send)
+    drain(near_cap.at[near_slab], n_send.at[2])
+
+    @pl.when(near_there)
+    def _():
+        for k in (0, 1):
+            drain(near_cap.at[near_slab], n_send.at[k])
+
     for d in range(1, layers):
         drain(caps[0].at[own_slab], c_send.at[d])
     for d in range(layers):
@@ -1160,7 +1193,6 @@
         vmem(half, steps),
         vmem(wide, 2 * slots, 2),
         vmem(slots, wide, 3),
-        vmem(wide, 2),
         vmem(wide, slots, 2),
         vmem(slots, quarter),
         vmem(slabs * quarter),
@@ -1172,19 +1204,16 @@
         vmem(half, steps),
         vmem(half, 2, steps),
         pltpu.SMEM(table.shape, jnp.float32),
-        *[vmem(n, 2) for n in extents[1:]],
-        vmem(extent + 2 * HALO),
-        *[vmem(n) for n in extents[1:]],
-        *[vmem(n, 3) for n in extents[1:]],
-        *[vmem(n + 2, 2) for n in extents[1:]],
-        *[vmem(n + 2, 2) for n in extents[1:]],
-        sems(thick + 1),
-        sems(half, 2),
+        vmem(6 * thick),
+        *[vmem(n) for n in extents],
+        *[vmem(n // 2, 4) for n in extents[1:]],
+        sems(thick + 2),
+        sems(half, PARTS, 2),
+        sems(half, PARTS),
         sems(half),
         sems(half),
-        sems(half),
-        sems(half),
-        sems(half),
+        sems(half, PARTS),
+        sems(half, PARTS),
         sems(half),
         sems(half),
         sems(HALO, 2),
@@ -1197,12 +1226,14 @@
         sems(slots),
         one,
         one,
-        sems(half),
-        sems(half),
-        sems(half, 2),
-        sems(2, half),
+        sems(half, PARTS),
+        sems(half, PARTS),
+        sems(half, PARTS, 2),
+        sems(2, half, PARTS),
         sems(2 * layers),
         sems(2 * layers),
+        sems(3),
+        sems(3),
         pltpu.SemaphoreType.REGULAR((layers - 1,)),
     ]
     return pl.pallas_call(
@@ -1217,7 +1248,7 @@
         compiler_params=pltpu.CompilerParams(
             collective_id=0, has_side_effects=True, vmem_limit_bytes=32 * 2**20
         ),
-    )(residual, capacity)
+    )(*[pltpu.with_memory_space_constraint(a, pltpu.HBM) for a in (residual, capacity)])
 
 
 def fits_fused(groups, slabs, residual):
@@ -1230,7 +1261,7 @@
         and slabs % 2 == 0
         and slabs == length // 8
         and thick == 8
-        and all(n % 2 == 0 and n % min(n, BLOCK) == 0 for n in level_extents(slabs * thick))
+        and all(n % 2 == 0 and n % n == 0 for n in level_extents(slabs * thick))
         and (second, third) == (8, 128)
     )
 

time: 47.5 us -> 42.6 us (0.90)
  Pallas kernels: 44.7 us -> 41.6 us
  local copies, waits for them, and re-layouts: 2.59 us -> 0.8 us
    pallas_call x1, Pallas kernels: 44.7 us -> 41.6 us  [fused(): pl.pallas_call(functools.partial(whole_kernel, groups, slabs, table), out...]
    unnamed x5 -> x1, local copies, waits for them, and re-layouts: 2.59 us -> 0.8 us
where the time goes in v2:
time: 42.6 us; the launch traced here: 42.4 us
  Pallas kernels  41.6 us (98%)
  local copies, waits for them, and re-layouts  0.8 us (2%)
    pallas_call x1, Pallas kernels, fused(): pl.pallas_call(functools.partial(whole_kernel, groups, slabs, table), out...  41.6 us

profile of v2, /device:TPU:1, one launch (start us, length us, event | category | flops | bytes accessed | tf_op | source)
XLA Modules:
  0.0 42.4 jit_solution(11073355319548047985)
XLA Ops:
  0.0 41.6 %shard_map.28 = f32[16,8,8,128]{3,2,1,0:T(8,128)S(1)} custom-call(f32[16,8,8,128]{3,2,1,0:T(8,128)} %residual_hbm.1, f32[8,8,128]{2,1,0:T(8,128)} %capacity_hbm.1), custom_call_target="tpu_custom_call" | custom-call | tf_op jit(solution)/shard_map/pallas_call | solution.py:1239
  41.6 0.8 %copy.4 = f32[16,8,8,128]{3,2,1,0:T(8,128)} copy(f32[16,8,8,128]{3,2,1,0:T(8,128)S(1)} %shard_map.28) | data formatting | bytes 1048576

commit v3 on v2

--- a/solution.py
+++ b/solution.py
@@ -575,18 +575,13 @@
             device_id_type=MESH,
         ).start()
 
-    takes = []
-    for i in range(half):
-        for h in (0, 1):
-            p = plane_of(h, i)
-            copy = pltpu.make_async_copy(residual_hbm.at[:, p], res.at[:, p], own.at[p])
-            copy.start()
-            takes.append((p, copy))
+    take_residual = pltpu.make_async_copy(residual_hbm, res, own.at[0])
+    take_residual.start()
     own_slab = pl.ds(s * thick, thick)
-    take_capacity = pltpu.make_async_copy(capacity_hbm, caps[0].at[own_slab], own.at[thick])
+    take_capacity = pltpu.make_async_copy(capacity_hbm, caps[0].at[own_slab], own.at[1])
     take_capacity.start()
     near_slab = pl.ds((2 + c) * thick, thick)
-    take_near = pltpu.make_async_copy(capacity_hbm, near_cap.at[near_slab], own.at[thick + 1])
+    take_near = pltpu.make_async_copy(capacity_hbm, near_cap.at[near_slab], own.at[2])
     take_near.start()
 
     barrier = pltpu.get_barrier_semaphore()
@@ -635,13 +630,8 @@
 
     pl.semaphore_wait(barrier, 4 + 2 * sides)
 
-    waited = {}
-    for p, copy in takes:
-        waited[p] = copy
-
+    take_residual.wait()
     for i in range(half):
-        for h in (0, 1):
-            waited[plane_of(h, i)].wait()
 
         @pl.when(keeper)
         def _():
@@ -650,11 +640,11 @@
 
                 @pl.when(side == h)
                 def _():
-                    pltpu.make_async_copy(res.at[:, p], loc.at[i], loc_recv.at[i]).start()
+                    pltpu.make_async_copy(res.at[:, p], loc.at[i], loc_recv).start()
 
                 @pl.when(side != h)
                 def _():
-                    send(res.at[:, p], loc.at[i], loc_send.at[i], loc_recv.at[i], at(y, x, z, 1 - c))
+                    send(res.at[:, p], loc.at[i], loc_send, loc_recv, at(y, x, z, 1 - c))
 
         @pl.when(jnp.logical_not(keeper))
         def _():
@@ -662,13 +652,13 @@
                 span = pl.ds(k * part_steps, part_steps)
                 for h in (0, 1):
                     send(
-                        res.at[span, plane_of(h, i)], far.at[i, span], far_send.at[i, k, h],
+                        res.at[span, plane_of(h, i)], far.at[i, span], far_send,
                         far_recv.at[i, k], at(1 - y, x, z, lax.rem(h + x, 2)),
                     )
 
     take_near.wait()
     send(
-        near_cap.at[near_slab], near_cap.at[near_slab], n_send.at[2], n_recv.at[2],
+        near_cap.at[near_slab], near_cap.at[near_slab], n_send.at[0], n_recv.at[2],
         at(y, x, z, 1 - c),
     )
     near_there = jnp.where(c == 0, below, above)
@@ -679,7 +669,7 @@
             send(
                 near_cap.at[near_slab],
                 near_cap.at[pl.ds((4 - 3 * c) * thick, thick)],
-                n_send.at[k],
+                n_send.at[1],
                 n_recv.at[1 - c],
                 at(y, x, z + 2 * c - 1, k),
             )
@@ -702,7 +692,7 @@
             send(
                 caps[0].at[own_slab],
                 caps[0].at[own_slab],
-                c_send.at[d],
+                c_send,
                 c_recv.at[d],
                 (m, lax.rem(s + 2 * d, slabs)),
             )
@@ -716,8 +706,8 @@
         send(
             caps[0].at[rows],
             caps[0].at[rows],
-            c_send.at[layers + d],
-            c_recv.at[layers + d],
+            c_send,
+            c_recv.at[0],
             at(y, x, z, 1 - c),
         )
 
@@ -736,7 +726,8 @@
     give_far = jnp.where(first_x, -sign * there_power, there_power)
 
     def combine(i):
-        drain(loc.at[i], loc_recv.at[i])
+        if i == 0:
+            drain(loc, loc_recv)
         for k in range(PARTS):
             span = pl.ds(k * part_steps, part_steps)
             drain(far.at[i, span], far_recv.at[i, k])
@@ -746,7 +737,7 @@
             send(
                 sendx.at[i, span],
                 seq.at[i, pl.ds(x * steps + k * part_steps, part_steps)],
-                x_send.at[i, k],
+                x_send,
                 x_recv.at[i, k],
                 at(y, 1 - x, z, 1 - c),
             )
@@ -781,7 +772,7 @@
                 field[plane, k, 1] = modes[k][1]
 
         given = field.at[plane, pl.ds((1 - c) * slots, slots)]
-        send(given, given, d_send.at[i], d_recv.at[i], at(y, x, z, 1 - c))
+        send(given, given, d_send, d_recv, at(y, x, z, 1 - c))
         if i < HALO:
             target = plane + thick * (1 - 2 * side)
 
@@ -792,8 +783,8 @@
                     send(
                         field.at[plane, part],
                         field.at[target, part],
-                        h_send.at[i, k],
-                        h_recv.at[1 - side, i],
+                        h_send,
+                        h_recv.at[1 - side],
                         at(halo_y, x, halo_z, k),
                     )
 
@@ -801,7 +792,7 @@
         return tuple(table[slot, column] for column in range(3))
 
     even_row, even_lane = parity(tile, 0), parity(tile, 1)
-    solver_shifts = shifts_of(x * 2 * slots + c * slots + slab)
+    solver_shifts = shifts_of(x * 2 * slots + (1 - c) * slots + slab)
 
     def pass_capacity():
         for d in range(1, layers):
@@ -809,8 +800,7 @@
             forward_cap(d)
 
     def coarse_tables():
-        for d in range(layers):
-            drain(caps[0].at[own_slab], c_recv.at[layers + d])
+        drain(caps[0].at[pl.ds(0, layers * thick)], c_recv.at[0])
         for level in range(1, depth):
             caps[level][...] = block_mean(caps[level - 1][...], 2 ** (level - 1))
             compact_table(level, caps[level], tables[level], solver_shifts, even_row)
@@ -855,9 +845,11 @@
             combine(turn - 1)
         hear_sides(turn)
     share_capacity()
-    for i in range(layers - 2, half):
+    for i in range(layers - 2, half - 1):
         combine(i)
-    for i in range(half):
+    transform(0)
+    combine(half - 1)
+    for i in range(1, half):
         transform(i)
         if i == 1:
             fine_tables()
@@ -876,16 +868,16 @@
 
     def member(g):
         gz, gs = g // 2, lax.rem(g, 2)
-        return at(lax.rem(gs + gz, 2), x, gz, c)
-
-    for i in range(half):
-        drain(field.at[0, pl.ds(0, slots)], d_recv.at[i])
+        return at(lax.rem(gs + gz, 2), x, gz, 1 - c)
+
+    given_planes = field.at[pl.ds(0, half), pl.ds(0, slots)]
+    halo_planes = field.at[pl.ds(0, HALO), pl.ds(0, slots)]
+    drain(given_planes, d_recv)
     for end, there in ((0, jnp.logical_not(is_low)), (1, jnp.logical_not(is_high))):
 
         @pl.when(there)
         def _():
-            for i in range(HALO):
-                drain(field.at[0, pl.ds(0, slots)], h_recv.at[end, i])
+            drain(halo_planes, h_recv.at[end])
 
     def load_slot(f):
         q = c * slots + f
@@ -936,15 +928,7 @@
 
         tiles = pl.ds(slab * (thick // 4), thick // 4)
         for f in chosen:
-
-            @pl.when(f != slab)
-            def _():
-                send(coarse_out.at[f], gathered.at[tiles], g_send, g_recv, member(f))
-
-            @pl.when(f == slab)
-            def _():
-                for pair in range(thick // 4):
-                    gathered[slab * (thick // 4) + pair] = coarse_out[f, pair]
+            send(coarse_out.at[f], gathered.at[tiles], g_send, g_recv, member(f))
 
         return carry
 
@@ -967,8 +951,7 @@
         )
 
     coarse_tables()
-    others = gathered.at[pl.ds(0, (slabs - 1) * (thick // 4))]
-    drain(others, g_recv)
+    drain(gathered, g_recv)
     tiles_in = slabs * thick // 4
     unpacked = []
     for j in range(tiles_in):
@@ -988,16 +971,14 @@
     span = thick // 4 + 1
 
     def give(i, carry):
-        g = slot_at(slots - i)
+        g = slot_at(slots - 1 - i)
         send(
             back.at[pl.ds(g * (thick // 4), span)], edges.at[slab], b_send, b_recv.at[slab],
             member(g),
         )
         return carry
 
-    lax.fori_loop(1, slots, give, 0)
-    for k in range(span):
-        edges[slab, k] = back[slab * (thick // 4) + k]
+    lax.fori_loop(0, slots, give, 0)
 
     for end, there in ((0, jnp.logical_not(is_low)), (1, jnp.logical_not(is_high))):
 
@@ -1008,11 +989,8 @@
 
     def up(i, carry):
         chosen = [slot_at(TOGETHER * i + k) for k in range(TOGETHER)]
-        for k, f in enumerate(chosen):
-
-            @pl.when(TOGETHER * i + k > 0)
-            def _():
-                drain(edges.at[0], b_recv.at[f])
+        for f in chosen:
+            drain(edges.at[0], b_recv.at[f])
 
         loaded = [load_slot(f) for f in chosen]
         start = [[] for f in chosen]
@@ -1061,7 +1039,7 @@
         for k in range(PARTS):
             send(
                 wave.at[i, pl.ds((1 - x) * steps + k * part_steps, part_steps)],
-                gotb.at[i, pl.ds(k * part_steps, part_steps)], w_send.at[i, k], w_recv.at[i, k],
+                gotb.at[i, pl.ds(k * part_steps, part_steps)], w_send, w_recv.at[i, k],
                 at(y, 1 - x, z, 1 - c),
             )
 
@@ -1079,10 +1057,10 @@
         for t in range(k * part_steps, (k + 1) * part_steps):
             mine = wave[i, x * steps + t] * (rate**-t)
             got = gotb[i, t] * (rate**-t)
-            outgoing[i, 1, t] = (far_own * inverse_there) * mine + (far_got * inverse_there) * got
+            outgoing[1, i, t] = (far_own * inverse_there) * mine + (far_got * inverse_there) * got
         send(
-            outgoing.at[i, 1, span], out_ref.at[span, p], o_send.at[i, k, 1],
-            o_recv.at[side, i, k], at(1 - y, x, z, sig),
+            outgoing.at[1, i, span], out_ref.at[span, p], o_send.at[1], o_recv,
+            at(1 - y, x, z, sig),
         )
 
         def own_value(t):
@@ -1098,10 +1076,10 @@
         @pl.when(jnp.logical_not(keeper))
         def _():
             for t in range(k * part_steps, (k + 1) * part_steps):
-                outgoing[i, 0, t] = own_value(t)
+                outgoing[0, i, t] = own_value(t)
             send(
-                outgoing.at[i, 0, span], out_ref.at[span, p], o_send.at[i, k, 0],
-                o_recv.at[side, i, k], at(y, x, z, 1 - c),
+                outgoing.at[0, i, span], out_ref.at[span, p], o_send.at[0], o_recv,
+                at(y, x, z, 1 - c),
             )
 
     for i in range(half):
@@ -1110,52 +1088,36 @@
         for k in range(PARTS):
             finish(i, k)
 
-    block = loc.at[0]
-    piece = loc.at[0, pl.ds(0, part_steps)]
-    for i in range(half):
-        for k in range(PARTS):
-
-            @pl.when(keeper)
-            def _():
-                drain(piece, o_recv.at[1 - side, i, k])
-
-            @pl.when(jnp.logical_not(keeper))
-            def _():
-                for h in (0, 1):
-                    drain(piece, o_recv.at[h, i, k])
-                    drain(piece, far_send.at[i, k, h])
-                drain(piece, o_send.at[i, k, 0])
-
-            drain(piece, o_send.at[i, k, 1])
-            drain(piece, x_send.at[i, k])
-            drain(piece, w_send.at[i, k])
-
-        @pl.when(keeper)
-        def _():
-            drain(block, loc_send.at[i])
-
-        drain(field.at[0, pl.ds(0, slots)], d_send.at[i])
-        if i < HALO:
-
-            @pl.when(halo_there)
-            def _():
-                for k in (0, 1):
-                    drain(field.at[0, pl.ds(0, slots)], h_send.at[i, k])
-
-    drain(others, g_send)
-    drain(edges.at[pl.ds(0, slots - 1)], b_send)
+    @pl.when(keeper)
+    def _():
+        drain(loc, o_recv)
+        drain(loc, loc_send)
+
+    @pl.when(jnp.logical_not(keeper))
+    def _():
+        drain(res, o_recv)
+        drain(res, far_send)
+        drain(loc, o_send.at[0])
+
+    drain(loc, o_send.at[1])
+    drain(loc, x_send)
+    drain(loc, w_send)
+    drain(given_planes, d_send)
+
+    @pl.when(halo_there)
+    def _():
+        drain(field.at[pl.ds(0, 2 * HALO), pl.ds(0, slots)], h_send)
+
+    drain(gathered, g_send)
+    drain(edges, b_send)
     drain(merged.at[pl.ds(0, slots)], r_send)
-    drain(near_cap.at[near_slab], n_send.at[2])
+    drain(near_cap.at[near_slab], n_send.at[0])
 
     @pl.when(near_there)
     def _():
-        for k in (0, 1):
-            drain(near_cap.at[near_slab], n_send.at[k])
-
-    for d in range(1, layers):
-        drain(caps[0].at[own_slab], c_send.at[d])
-    for d in range(layers):
-        drain(caps[0].at[own_slab], c_send.at[layers + d])
+        drain(near_cap.at[pl.ds(0, 2 * thick)], n_send.at[1])
+
+    drain(caps[0].at[pl.ds(0, (2 * layers - 1) * thick)], c_send)
 
 
 def level_extents(extent):
@@ -1202,37 +1164,37 @@
         vmem(2 * slots, half, 2),
         vmem(half, 2 * steps),
         vmem(half, steps),
-        vmem(half, 2, steps),
+        vmem(2, half, steps),
         pltpu.SMEM(table.shape, jnp.float32),
         vmem(6 * thick),
         *[vmem(n) for n in extents],
         *[vmem(n // 2, 4) for n in extents[1:]],
-        sems(thick + 2),
-        sems(half, PARTS, 2),
+        sems(3),
+        one,
         sems(half, PARTS),
-        sems(half),
-        sems(half),
+        one,
+        one,
+        one,
         sems(half, PARTS),
-        sems(half, PARTS),
-        sems(half),
-        sems(half),
-        sems(HALO, 2),
-        sems(2, HALO),
+        one,
+        one,
+        one,
         sems(2),
         sems(2),
+        sems(2),
         one,
         one,
         one,
         sems(slots),
         one,
         one,
+        one,
         sems(half, PARTS),
-        sems(half, PARTS),
-        sems(half, PARTS, 2),
-        sems(2, half, PARTS),
-        sems(2 * layers),
-        sems(2 * layers),
-        sems(3),
+        sems(2),
+        one,
+        one,
+        sems(layers),
+        sems(2),
         sems(3),
         pltpu.SemaphoreType.REGULAR((layers - 1,)),
     ]

time: 42.6 us -> 40 us (0.939)
  Pallas kernels: 41.6 us -> 39.1 us
    pallas_call x1, Pallas kernels: 41.6 us -> 39.1 us  [fused(): pl.pallas_call(functools.partial(whole_kernel, groups, slabs, table), out...]
where the time goes in v3:
time: 40 us; the launch traced here: 39.9 us
  Pallas kernels  39.1 us (98%)
  local copies, waits for them, and re-layouts  0.8 us (2%)
    pallas_call x1, Pallas kernels, fused(): pl.pallas_call(functools.partial(whole_kernel, groups, slabs, table), out...  39.1 us

profile of v3, /device:TPU:1, one launch (start us, length us, event | category | flops | bytes accessed | tf_op | source)
XLA Modules:
  0.0 39.9 jit_solution(16845175526913460537)
XLA Ops:
  0.0 39.1 %shard_map.28 = f32[16,8,8,128]{3,2,1,0:T(8,128)S(1)} custom-call(f32[16,8,8,128]{3,2,1,0:T(8,128)} %residual_hbm.1, f32[8,8,128]{2,1,0:T(8,128)} %capacity_hbm.1), custom_call_target="tpu_custom_call" | custom-call | tf_op jit(solution)/shard_map/pallas_call | solution.py:1201
  39.1 0.8 %copy.4 = f32[16,8,8,128]{3,2,1,0:T(8,128)} copy(f32[16,8,8,128]{3,2,1,0:T(8,128)S(1)} %shard_map.28) | data formatting | bytes 1048576

commit v4 on v3

--- a/solution.py
+++ b/solution.py
@@ -397,26 +397,27 @@
     return found
 
 
-def neighbour_sum(below, here, above, weights):
-    along_first, masked, distance = weights
-    total = along_first[0] * above + along_first[1] * below
+def around(value, weights):
+    unused, masked, distance = weights
+    total = 0.0
     for dim in (0, 1):
         upper, lower = masked[dim]
-        total = total + upper * shifted(here, -distance, dim)
-        total = total + lower * shifted(here, distance, dim)
+        total = total + upper * shifted(value, -distance, dim)
+        total = total + lower * shifted(value, distance, dim)
     return total
 
 
-def updated(forcing, inverse, columns, weights):
-    results, rest = [], []
-    for part in (0, 1):
-        below, here, above = (column[part] for column in columns)
-        rest.append(forcing[part] - neighbour_sum(below, here, above, weights))
+def smoothed(first, columns, inverse, weights):
+    ahead, behind = weights[0]
+    below, here, above = columns
+    n0, n1 = (
+        ahead * above[k] + behind * below[k] + around(here[k], weights) for k in (0, 1)
+    )
     a, b, c = inverse
-    r0, r1 = rest
-    results.append((1.0 - OMEGA) * columns[1][0] + (a * r0 + b * r1))
-    results.append((1.0 - OMEGA) * columns[1][1] + (c * r1 - b * r0))
-    return results
+    return (
+        first[0] + (1.0 - OMEGA) * here[0] - (a * n0 + b * n1),
+        first[1] + (1.0 - OMEGA) * here[1] - (c * n1 - b * n0),
+    )
 
 
 def compact_rest(forcing, values, weights, even_row):
@@ -526,11 +527,11 @@
 
 def whole_kernel(groups, slabs, shift_table, residual_hbm, capacity_hbm, out_ref, *scratch):
     (
-        res, loc, far, seq, sendx, field, inverse0, vtwo, coarse_out, gathered, back, edges,
+        res, loc, far, seq, sendx, field, inverse0, vone, vtwo, coarse_out, gathered, back, edges,
         result, merged, wave, gotb, outgoing, table, near_cap,
-    ) = scratch[:19]
+    ) = scratch[:20]
     depth = GRID_DEPTH
-    rest = scratch[19:]
+    rest = scratch[20:]
     caps, rest = rest[:depth], rest[depth:]
     tables, rest = (None,) + rest[: depth - 1], rest[depth - 1 :]
     (
@@ -879,50 +880,56 @@
         def _():
             drain(halo_planes, h_recv.at[end])
 
-    def load_slot(f):
-        q = c * slots + f
-        forcing = [(field[j, q, 0], field[j, q, 1]) for j in range(wide)]
-        inverse = [[inverse0[f, j, k] for k in range(3)] for j in range(wide)]
-        return forcing, inverse
-
-    def residual_at(forcing, second, j, shifts):
+    def load_inverse(f):
+        return [[inverse0[f, j, k] for k in range(3)] for j in range(wide)]
+
+    def residual_pair(forcing, second, j, shifts):
         s1, s2, s3 = shifts
-        cap = near_cap[cap_base + j]
-        re, im = second[j]
-        turn = (s1 * re - s2 * im, s2 * re + s3 * im)
+        ahead, behind = weights[0]
+        turned_sums = [0.0, 0.0]
+        for k in (j, j + 1):
+            re, im = second[k]
+            cap = near_cap[cap_base + k]
+            top, coupling, bottom = 6.0 * spread0 + cap * s1, cap * s2, 6.0 * spread0 + cap * s3
+            turned_sums[0] = turned_sums[0] + (top * re - coupling * im)
+            turned_sums[1] = turned_sums[1] + (coupling * re + bottom * im)
         found = []
         for part in (0, 1):
-            total = forcing[j][part] - neighbour_sum(
-                *(second[n][part] for n in (j - 1, j, j + 1)), weights
-            )
-            found.append(total - (6.0 * spread0 * second[j][part] + cap * turn[part]))
+            near = [second[k][part] for k in (j - 1, j, j + 1, j + 2)]
+            total = ahead * (near[2] + near[3]) + behind * (near[0] + near[1])
+            total = total + around(near[1] + near[2], weights) + turned_sums[part]
+            found.append(forcing[j][part] + forcing[j + 1][part] - total)
         return found
 
     def down(i, carry):
         chosen = [slot_at(slots - 1 - TOGETHER * i - k) for k in range(TOGETHER)]
-        loaded = [load_slot(f) for f in chosen]
+        forcings = [
+            [(field[j, c * slots + f, 0], field[j, c * slots + f, 1]) for j in range(wide)]
+            for f in chosen
+        ]
+        inverses = [load_inverse(f) for f in chosen]
         shifts = [shifts_of(x * 2 * slots + c * slots + f) for f in chosen]
         first = [[] for f in chosen]
         second = [[None] for f in chosen]
         for j in range(wide):
-            for n, (forcing, inverse) in enumerate(loaded):
-                (re, im), (a, b, d) = forcing[j], inverse[j]
+            for n, f in enumerate(chosen):
+                (re, im), (a, b, d) = forcings[n][j], inverses[n][j]
                 first[n].append((a * re + b * im, d * im - b * re))
+                for part in (0, 1):
+                    vone[j, f, part] = first[n][j][part]
         for j in range(1, wide - 1):
-            for n, (forcing, inverse) in enumerate(loaded):
-                second[n].append(updated(forcing[j], inverse[j], first[n][j - 1 : j + 2], weights))
+            for n, f in enumerate(chosen):
+                second[n].append(
+                    smoothed(first[n][j], first[n][j - 1 : j + 2], inverses[n][j], weights)
+                )
                 for part in (0, 1):
-                    vtwo[j, chosen[n], part] = second[n][j][part]
+                    vtwo[j, f, part] = second[n][j][part]
         for pair in range(thick // 4):
-            packed = [[[None, None], [None, None]] for f in chosen]
+            packed = [[None, None] for f in chosen]
             for plane in (0, 1):
-                for k in (0, 1):
-                    for n, (forcing, inverse) in enumerate(loaded):
-                        j = HALO + 4 * pair + 2 * plane + k
-                        rest = residual_at(forcing, second[n], j, shifts[n])
-                        for part in (0, 1):
-                            sofar = packed[n][plane][part]
-                            packed[n][plane][part] = rest[part] if k == 0 else sofar + rest[part]
+                for n, f in enumerate(chosen):
+                    j = HALO + 4 * pair + 2 * plane
+                    packed[n][plane] = residual_pair(forcings[n], second[n], j, shifts[n])
             for n, f in enumerate(chosen):
                 coarse_out[f, pair] = 0.125 * pack_means(*packed[n], even_row, even_lane)
 
@@ -992,7 +999,7 @@
         for f in chosen:
             drain(edges.at[0], b_recv.at[f])
 
-        loaded = [load_slot(f) for f in chosen]
+        inverses = [load_inverse(f) for f in chosen]
         start = [[] for f in chosen]
         third = [[None] for f in chosen]
         for k in range(span):
@@ -1001,13 +1008,15 @@
                     for j in (4 * k + 2 * u, 4 * k + 2 * u + 1):
                         start[n].append([vtwo[j, f, part] + extra[part] for part in (0, 1)])
         for j in range(1, wide - 1):
-            for n, (forcing, inverse) in enumerate(loaded):
-                third[n].append(updated(forcing[j], inverse[j], start[n][j - 1 : j + 2], weights))
+            for n, f in enumerate(chosen):
+                first = (vone[j, f, 0], vone[j, f, 1])
+                third[n].append(smoothed(first, start[n][j - 1 : j + 2], inverses[n][j], weights))
         for j in range(HALO, wide - HALO):
-            for n, (forcing, inverse) in enumerate(loaded):
-                parts = updated(forcing[j], inverse[j], third[n][j - 1 : j + 2], weights)
+            for n, f in enumerate(chosen):
+                first = (vone[j, f, 0], vone[j, f, 1])
+                parts = smoothed(first, third[n][j - 1 : j + 2], inverses[n][j], weights)
                 for part in (0, 1):
-                    result[chosen[n], j - HALO, part] = parts[part]
+                    result[f, j - HALO, part] = parts[part]
         for f in chosen:
             q = c * slots + f
             send(
@@ -1155,6 +1164,7 @@
         vmem(half, steps),
         vmem(wide, 2 * slots, 2),
         vmem(slots, wide, 3),
+        vmem(wide, slots, 2),
         vmem(wide, slots, 2),
         vmem(slots, quarter),
         vmem(slabs * quarter),

time: 40 us -> 39.8 us (level)
  no operation moved by 1% of the time
where the time goes in v4:
time: 39.8 us; the launch traced here: 39.7 us
  Pallas kernels  38.9 us (98%)
  local copies, waits for them, and re-layouts  0.8 us (2%)
    pallas_call x1, Pallas kernels, fused(): pl.pallas_call(functools.partial(whole_kernel, groups, slabs, table), out...  38.9 us

profile of v4, /device:TPU:1, one launch (start us, length us, event | category | flops | bytes accessed | tf_op | source)
XLA Modules:
  0.0 39.7 jit_solution(15056327716141072206)
XLA Ops:
  0.0 38.9 %shard_map.28 = f32[16,8,8,128]{3,2,1,0:T(8,128)S(1)} custom-call(f32[16,8,8,128]{3,2,1,0:T(8,128)} %residual_hbm.1, f32[8,8,128]{2,1,0:T(8,128)} %capacity_hbm.1), custom_call_target="tpu_custom_call" | custom-call | tf_op jit(solution)/shard_map/pallas_call | solution.py:1211
  38.9 0.8 %copy.4 = f32[16,8,8,128]{3,2,1,0:T(8,128)} copy(f32[16,8,8,128]{3,2,1,0:T(8,128)S(1)} %shard_map.28) | data formatting | bytes 1048576

commit v5 on v4

--- a/solution.py
+++ b/solution.py
@@ -939,7 +939,8 @@
 
         return carry
 
-    lax.fori_loop(0, slots // TOGETHER, down, 0)
+    for turn in range(slots // TOGETHER):
+        down(turn, 0)
 
     low_y, low_z = jnp.where(sig == 0, y, 1 - y), jnp.where(sig == 0, z - 1, z)
     high_y, high_z = jnp.where(sig == 0, 1 - y, y), jnp.where(sig == 0, z, z + 1)
@@ -985,7 +986,8 @@
         )
         return carry
 
-    lax.fori_loop(0, slots, give, 0)
+    for turn in range(slots):
+        give(turn, 0)
 
     for end, there in ((0, jnp.logical_not(is_low)), (1, jnp.logical_not(is_high))):
 

time: 39.8 us -> 39.7 us (level)
  no operation moved by 1% of the time
where the time goes in v5:
time: 39.7 us; the launch traced here: 39.5 us
  Pallas kernels  38.7 us (97%)
  local copies, waits for them, and re-layouts  0.8 us (2%)
    pallas_call x1, Pallas kernels, fused(): pl.pallas_call(functools.partial(whole_kernel, groups, slabs, table), out...  38.7 us
    unnamed x1, local copies, waits for them, and re-layouts  0.8 us

profile of v5, /device:TPU:1, one launch (start us, length us, event | category | flops | bytes accessed | tf_op | source)
XLA Modules:
  0.0 39.5 jit_solution(2554155295904229716)
XLA Ops:
  0.0 38.7 %shard_map.28 = f32[16,8,8,128]{3,2,1,0:T(8,128)S(1)} custom-call(f32[16,8,8,128]{3,2,1,0:T(8,128)} %residual_hbm.1, f32[8,8,128]{2,1,0:T(8,128)} %capacity_hbm.1), custom_call_target="tpu_custom_call" | custom-call | tf_op jit(solution)/shard_map/pallas_call | solution.py:1213
  38.7 0.8 %copy.4 = f32[16,8,8,128]{3,2,1,0:T(8,128)} copy(f32[16,8,8,128]{3,2,1,0:T(8,128)S(1)} %shard_map.28) | data formatting | bytes 1048576
